TPU v7x, 256 devices: a whole 4x4x8 slice. The times are simulated.
256 devices in a mesh: member: 8 (over z_hi, core), space: 16 (over x, y), group: 2 (over z_lo).
Axes of the slice: x: 4, y: 4, z: 8 (z_hi: 4, z_lo: 2; z = z_hi * 2 + z_lo), core: 2. Of those that a mesh axis runs over, the one named last changes fastest.
Arguments:
- ensemble: bfloat16 [2, 512, 3, 64, 512], P('group', 'member', None, 'space'), may hold values from -6 to 6
- obs_index: int32 [2, 16, 8, 256], P('group', 'space'), may hold values from 0 to 255
- obs_value: float32 [2, 16, 8, 256], P('group', 'space', 'member'), may hold values from -6 to 6
- obs_var: float32 [2, 16, 8, 256], P('group', 'space', 'member'), may hold values from 0.3 to 3
Outputs:
- analysis: bfloat16 [2, 512, 3, 64, 512], P('group', 'member', None, 'space')
Inputs may be any that keep to these rules, and one draw needn't show every extreme that they name: `obs_index`: each entry names a cell of its region's tile, counted row by row over 64 columns; cells may repeat.
All inputs are finite; a program needn't handle non-finite values.
Results may differ from a plain program's by a relative error of at most 0.0075.
Values may be sent and summed in bfloat16 or wider, within the bound.
No kernel may reach another device: no remote copies, remote signals or barrier semaphores. Data moves between devices by JAX's collectives and lax.ppermute only.
A program may use at most 64 MiB of HBM per device.

v0:
```python
import functools
import math

import jax
import jax.numpy as jnp
from jax import lax
from jax.experimental import pallas as pl
from jax.experimental.pallas import tpu as pltpu
from jax.sharding import PartitionSpec as P

NS_STEPS = 6
MEMBERS = 512
CELLS = 256
OBS = 256
BLOCK = 128
PAIRS = [(i, j) for i in range(4) for j in range(i, 4)]
CENTRE_AT = len(PAIRS) * BLOCK
PACKED = CENTRE_AT + 4 * 16

time_step = 0.4
coriolis = 0.3
COLS = 768
HALF = 384
HALVES = 1
PARTS = 2
f32 = jnp.float32
bf16 = jnp.bfloat16
vmem = pl.BlockSpec(memory_space=pltpu.VMEM)
smem = pl.BlockSpec(memory_space=pltpu.SMEM)


def column_difference(field):
    columns = field.shape[-1]
    return 0.5 * (pltpu.roll(field, columns - 1, 1) - pltpu.roll(field, 1, 1))


def rates(h, v, u, i):
    d_height = -(column_difference(u[i]) + 0.5 * (v[i + 1] - v[i - 1]))
    d_north = -0.5 * (h[i + 1] - h[i - 1]) - coriolis * u[i]
    return d_height, d_north


def rate_east(h, v, i):
    return coriolis * v[i] - column_difference(h[i])


def advance(h0, v0, u0):
    h1, v1, u1, h2, v2, u2, h3, v3, u3 = ({} for _ in range(9))
    for i in range(-2, 6):
        dh, dv = rates(h0, v0, u0, i)
        h1[i] = h0[i] + time_step * dh
        v1[i] = v0[i] + time_step * dv
        if -1 <= i <= 4:
            u1[i] = u0[i] + time_step * rate_east(h0, v0, i)
    for i in range(-1, 5):
        dh, dv = rates(h1, v1, u1, i)
        h2[i] = 0.75 * h0[i] + 0.25 * (h1[i] + time_step * dh)
        v2[i] = 0.75 * v0[i] + 0.25 * (v1[i] + time_step * dv)
        if 0 <= i <= 3:
            u2[i] = 0.75 * u0[i] + 0.25 * (u1[i] + time_step * rate_east(h1, v1, i))
    third = 1.0 / 3.0
    two_thirds = 2.0 / 3.0
    for i in range(4):
        dh, dv = rates(h2, v2, u2, i)
        h3[i] = h0[i] * third + two_thirds * (h2[i] + time_step * dh)
        v3[i] = v0[i] * third + two_thirds * (v2[i] + time_step * dv)
        u3[i] = u0[i] * third + two_thirds * (u2[i] + time_step * rate_east(h2, v2, i))
    return h3, v3, u3


GROUP = 16


def loaded(now, below, above, at):
    h, v, u = {}, {}, {}
    for f, field in enumerate((h, v, u)):
        for i in range(4):
            field[i] = now[f, i, at, :].astype(f32)
    for k in range(3):
        h[k - 3] = below[k, at, :].astype(f32)
        v[k - 3] = below[3 + k, at, :].astype(f32)
        h[4 + k] = above[k, at, :].astype(f32)
        v[4 + k] = above[3 + k, at, :].astype(f32)
    for k in range(2):
        u[k - 2] = below[6 + k, at, :].astype(f32)
        u[4 + k] = above[6 + k, at, :].astype(f32)
    return h, v, u


def first_step_kernel(now, below, above, out, first, last):
    def group(g, carry):
        at = pl.ds(pl.multiple_of(g * GROUP, GROUP), GROUP)
        fields = advance(*loaded(now, below, above, at))
        for f in range(3):
            edge = 2 if f == 2 else 3
            for i in range(4):
                out[f, i, at, :] = fields[f][i]
                if i < edge:
                    first[3 * f + i, at, :] = fields[f][i].astype(bf16)
                if i >= 4 - edge:
                    last[3 * f + i - (4 - edge), at, :] = fields[f][i].astype(bf16)
        return carry

    lax.fori_loop(0, now.shape[2] // GROUP, group, 0)


def last_step_kernel(base, now, below, above, *refs):
    out = refs[-1]
    lane = lax.broadcasted_iota(jnp.int32, (GROUP, BLOCK), 1) < 64

    def group(g, carry):
        at = pl.ds(pl.multiple_of(g * GROUP, GROUP), GROUP)
        into = pl.ds(pl.multiple_of(base + g * GROUP, GROUP), GROUP)
        fields = advance(*loaded(now, below, above, at))
        for f in range(3):
            for p in range(2):
                to = p * HALF + f * BLOCK
                for t in range(4):
                    x = fields[f][2 * p][:, t * BLOCK : (t + 1) * BLOCK]
                    y = fields[f][2 * p + 1][:, t * BLOCK : (t + 1) * BLOCK]
                    even = jnp.where(lane, x, pltpu.roll(y, 64, 1))
                    odd = jnp.where(lane, pltpu.roll(x, 64, 1), y)
                    out[2 * t, into, to : to + BLOCK] = even.astype(bf16)
                    out[2 * t + 1, into, to : to + BLOCK] = odd.astype(bf16)
        return carry

    lax.fori_loop(0, now.shape[2] // GROUP, group, 0)


def swapped(last, first, up, down):
    return lax.ppermute(last, "space", up), lax.ppermute(first, "space", down)


def edges(fields):
    last = jnp.concatenate([fields[0, 1:], fields[1, 1:], fields[2, 2:]], axis=0)
    first = jnp.concatenate([fields[0, :3], fields[1, :3], fields[2, :2]], axis=0)
    return last, first


def step(kernel, outs, *arrays, aliases={}):
    return pl.pallas_call(
        kernel,
        out_shape=outs,
        in_specs=[vmem] * len(arrays),
        out_specs=jax.tree.map(lambda _: vmem, outs),
        input_output_aliases=aliases,
        compiler_params=pltpu.CompilerParams(vmem_limit_bytes=12 * 1024 * 1024),
        cost_estimate=pl.CostEstimate(
            flops=100_000_000 // PARTS, bytes_accessed=1_000_000, transcendentals=0
        ),
    )(*arrays)


def forecast(fields, up, down):
    _, rows, members, columns = fields.shape
    half = members // PARTS
    now_shape = jax.ShapeDtypeStruct((3, rows, half, columns), f32)
    edge_shape = jax.ShapeDtypeStruct((8, half, columns), bf16)
    chunk_shape = jax.ShapeDtypeStruct((columns // 64, members, COLS), bf16)
    parts = [fields[:, :, n * half : (n + 1) * half] for n in range(PARTS)]
    halos = [swapped(*edges(part), up, down) for part in parts]
    first_outs = (now_shape, edge_shape, edge_shape)
    chunks = ()
    for n in range(PARTS):
        now, first, last = step(first_step_kernel, first_outs, parts[n], *halos[n])
        halo = swapped(last, first, up, down)
        kernel = functools.partial(last_step_kernel, n * half)
        aliases = {3: 0} if chunks else {}
        chunks = (step(kernel, chunk_shape, now, *halo, *chunks, aliases=aliases),)
    return chunks[0]


def dot(a, b):
    return jnp.dot(a, b, preferred_element_type=f32)


def dot_t(a, b):
    return lax.dot_general(a, b, (((1,), (1,)), ((), ())), preferred_element_type=f32)


def split(a):
    high = a.astype(bf16)
    return high, (a - high.astype(f32)).astype(bf16)


def product(a, b):
    return dot(a[0], b[0]) + (dot(a[0], b[1]) + dot(a[1], b[0]))


def eye(n):
    return (
        lax.broadcasted_iota(jnp.int32, (n, n), 0) == lax.broadcasted_iota(jnp.int32, (n, n), 1)
    ).astype(f32)


def total(a):
    return jnp.sum(jnp.sum(a, axis=1, keepdims=True), axis=0, keepdims=True)


def weights_kernel(*refs):
    regions = refs[:HALVES]
    tile, index, value, var, packed = refs[HALVES : HALVES + 5]
    z_ref, zt_ref, b_ref, m_ref, l_ref, u_ref = refs[HALVES + 5 :]
    identity = eye(OBS)

    def as_column(row):
        return jnp.sum(identity * row, axis=1, keepdims=True)

    index_row = index[pl.ds(tile[0], 1), :]
    index_col = as_column(index_row.astype(f32)).astype(jnp.int32)
    var_row = var[...]
    var_col = as_column(var_row)
    own = jnp.concatenate(
        [
            jnp.concatenate([part[:, :BLOCK], part[:, HALF : HALF + BLOCK]], axis=1)
            for part in regions
        ],
        axis=0,
    )
    cell_row = lax.broadcasted_iota(jnp.int32, (CELLS, OBS), 0)
    pick = (cell_row == index_row).astype(f32).astype(bf16)
    cell_col = lax.broadcasted_iota(jnp.int32, (OBS, CELLS), 1)
    pick_t = (cell_col == index_col).astype(f32).astype(bf16)
    y = dot(own, pick)
    mean_row = jnp.sum(y, axis=0, keepdims=True) * (1.0 / MEMBERS)
    inverse_row = lax.rsqrt(var_row)
    z_ref[...] = (y - mean_row) * inverse_row
    y_t = dot_t(pick_t, own)
    mean_col = jnp.sum(y_t, axis=1, keepdims=True) * (1.0 / MEMBERS)
    zt_ref[...] = (y_t - mean_col) * lax.rsqrt(var_col)
    w_row = (value[...] - mean_row) * inverse_row

    b = product(split(zt_ref[...]), split(z_ref[...]))
    diagonal = float(MEMBERS - 1)
    squared = diagonal * diagonal * MEMBERS + 2.0 * diagonal * total(b * identity) + total(b * b)
    inverse_norm = lax.rsqrt(squared)
    alpha = diagonal * inverse_norm
    b = b * inverse_norm
    b_ref[...] = b

    low = 1.5 - 0.5 * alpha
    lower = low * identity - 0.5 * b
    l_ref[...] = lower
    u_ref[...] = alpha * lower + product(split(b), split(lower))
    m_ref[...] = -0.5 * identity

    def one_step(_, low):
        identity = eye(OBS)
        m = m_ref[...]
        lower = l_ref[...]
        l_parts = split(lower)
        u_parts = split(u_ref[...])
        step = split(1.5 * identity - 0.5 * product(l_parts, u_parts))
        part = split(-0.5 * (low * (alpha * m + lower) + product(split(m), u_parts)))
        factor = 1.5 - 0.5 * alpha * low * low
        l_ref[...] = product(step, l_parts)
        m_ref[...] = factor * m + product(part, l_parts)
        u_ref[...] = product(step, u_parts)
        return factor * low

    low = lax.fori_loop(0, NS_STEPS - 2, one_step, low)
    m = m_ref[...]
    lower = l_ref[...]
    part = -0.5 * (low * (alpha * m + lower) + product(split(m), split(u_ref[...])))
    factor = 1.5 - 0.5 * alpha * low * low
    m = factor * m + product(split(part), split(lower))
    low = factor * low

    b = b_ref[...]
    once = low * w_row + jnp.sum(
        m * jnp.sum(b * w_row, axis=1, keepdims=True), axis=0, keepdims=True
    )
    inner = jnp.sum(b * once, axis=1, keepdims=True)
    once_col = jnp.sum(identity * once, axis=1, keepdims=True)
    inner_row = jnp.sum(identity * inner, axis=0, keepdims=True)
    twice = low * once_col + jnp.sum(m * inner_row, axis=1, keepdims=True)
    centre = jnp.sum(zt_ref[...] * twice, axis=0, keepdims=True) * inverse_norm

    scale = math.sqrt(diagonal) * jnp.sqrt(inverse_norm)
    m_parts = split(m * (scale * inverse_norm))
    small = eye(BLOCK)
    spot = lax.broadcasted_iota(jnp.int32, (16, BLOCK), 0)
    at = 0
    for i in range(4):
        v = product(split(z_ref[i * BLOCK : (i + 1) * BLOCK, :]), m_parts)
        band = product(split(v), split(zt_ref[:, i * BLOCK :]))
        for j in range(i, 4):
            block = band[:, (j - i) * BLOCK : (j - i + 1) * BLOCK]
            if i == j:
                block = block + (scale * low) * small
            packed[at : at + BLOCK, :] = block.astype(bf16)
            at += BLOCK
        piece = centre[:, i * BLOCK : (i + 1) * BLOCK]
        high = piece.astype(bf16).astype(f32)
        both = jnp.where(spot == 0, high, jnp.where(spot == 1, piece - high, 0.0))
        start = CENTRE_AT + 16 * i
        packed[start : start + 16, :] = both.astype(bf16)


def region_weights(regions, tile, index, values, variances):
    return pl.pallas_call(
        weights_kernel,
        out_shape=jax.ShapeDtypeStruct((PACKED, BLOCK), bf16),
        in_specs=[vmem] * HALVES + [smem] + [vmem] * 3,
        out_specs=pl.BlockSpec(memory_space=pltpu.VMEM),
        scratch_shapes=[
            pltpu.VMEM((MEMBERS, OBS), f32),
            pltpu.VMEM((OBS, MEMBERS), f32),
            pltpu.VMEM((OBS, OBS), f32),
            pltpu.VMEM((OBS, OBS), f32),
            pltpu.VMEM((OBS, OBS), f32),
            pltpu.VMEM((OBS, OBS), f32),
        ],
        compiler_params=pltpu.CompilerParams(vmem_limit_bytes=24 * 1024 * 1024),
        cost_estimate=pl.CostEstimate(flops=6_000_000_000, bytes_accessed=1_000_000, transcendentals=0),
        name="weights",
    )(
        *regions,
        tile,
        index,
        values,
        variances,
    )


def column_parts(columns, parity):
    place = lax.broadcasted_iota(jnp.int32, (1, columns), 1)
    row = 2 * (place // HALF) + (place // 64) % 2
    col = place % 64
    row_weight = jnp.abs((row.astype(f32) + 0.5) / 4.0 - 0.5)
    col_weight = jnp.abs((col.astype(f32) + 0.5) / 64.0 - 0.5)
    right = (col >= 32).astype(jnp.int32)
    sibling = ((right + parity) == 1).astype(f32)
    return row_weight, col_weight, sibling


def factors(parity):
    r, q, sibling = column_parts(COLS, parity)
    side = {0: 1.0 - q, 1: q * sibling, 2: q * (1.0 - sibling)}
    return {(row, s): (r if row else 1.0 - r) * side[s] for row in (0, 1) for s in (0, 1, 2)}


def unpack(source, base, full):
    for n, (i, j) in enumerate(PAIRS):
        block = source[base + n * BLOCK : base + (n + 1) * BLOCK, :]
        full[i * BLOCK : (i + 1) * BLOCK, j * BLOCK : (j + 1) * BLOCK] = block
        if i != j:
            turned = jnp.transpose(block.astype(f32)).astype(bf16)
            full[j * BLOCK : (j + 1) * BLOCK, i * BLOCK : (i + 1) * BLOCK] = turned


def apply(source, base, full, dev, acc, lo, hi, factor, before=None, out=None):
    unpack(source, base, full)
    shift = jnp.zeros((16, hi - lo), f32)
    for i in range(4):
        start = base + CENTRE_AT + 16 * i
        shift = shift + dot(source[start : start + 16, :], dev[i * BLOCK : (i + 1) * BLOCK, lo:hi])
    shift = jnp.sum(shift, axis=0, keepdims=True)
    factor = factor[:, lo:hi]
    wide = MEMBERS // HALVES // BLOCK
    slots = BLOCK * 8 // (MEMBERS // HALVES)
    size = BLOCK // slots

    def rows(i, carry):
        at = pl.ds(pl.multiple_of(i * BLOCK, BLOCK), BLOCK)
        term = factor * (dot(full[at, :], dev[:, lo:hi]) + shift)
        term = term + (acc[at, lo:hi] if before is None else before[:, lo:hi])
        if out is None:
            acc[at, lo:hi] = term
        else:
            tiles = pl.ds((i % wide) * slots, slots)
            spot = pl.ds(pl.multiple_of((i // wide) * size, size), size)
            out[tiles, spot, lo:hi] = term.astype(bf16).reshape(slots, size, hi - lo)
        return carry

    lax.fori_loop(0, 4, rows, 0)


def own_kernel(*refs):
    parity = refs[0]
    regions = refs[1 : 1 + HALVES]
    own, acc, dev, full, mean_ref = refs[1 + HALVES :]
    size = MEMBERS // HALVES
    for g in range(COLS // BLOCK):
        at = slice(g * BLOCK, (g + 1) * BLOCK)
        parts = [part[:, at].astype(f32) for part in regions]
        mean = sum(jnp.sum(part, axis=0, keepdims=True) for part in parts) * (1.0 / MEMBERS)
        mean_ref[:, at] = mean
        for n, part in enumerate(parts):
            dev[n * size : (n + 1) * size, at] = (part - mean).astype(bf16)
    apply(own, 0, full, dev, acc, 0, COLS, factors(parity[0])[0, 0], before=mean_ref)


def near_kernel(parity, acc_in, dev, sibling, other, below, above, acc, full):
    factor = factors(parity[0])
    apply(sibling, 0, full, dev, acc, 0, COLS, factor[0, 1])
    apply(other, 0, full, dev, acc, 0, COLS, factor[0, 2])
    apply(below, 0, full, dev, acc, 0, HALF, factor[1, 0])
    apply(above, 0, full, dev, acc, HALF, COLS, factor[1, 0])


def side_kernel(parity, acc_in, dev, below_sibling, above_sibling, acc, full):
    factor = factors(parity[0])
    apply(below_sibling, 0, full, dev, acc, 0, HALF, factor[1, 1])
    apply(above_sibling, 0, full, dev, acc, HALF, COLS, factor[1, 1])


def far_kernel(parity, acc, dev, below_other, above_other, out, full):
    factor = factors(parity[0])
    apply(below_other, 0, full, dev, acc, 0, HALF, factor[1, 2], out=out)
    apply(above_other, 0, full, dev, acc, HALF, COLS, factor[1, 2], out=out)


def call(kernel, outs, flops, scratch, parity, *arrays, alias=False):
    return pl.pallas_call(
    kernel,
    out_shape=outs,
    in_specs=[smem] + [vmem] * len(arrays),
    out_specs=jax.tree.map(lambda _: vmem, outs),
    scratch_shapes=[pltpu.VMEM((MEMBERS, MEMBERS), bf16)] + scratch,
    input_output_aliases={1: 0} if alias else {},
    compiler_params=pltpu.CompilerParams(vmem_limit_bytes=16 * 1024 * 1024),
    cost_estimate=pl.CostEstimate(flops=flops, bytes_accessed=1_000_000, transcendentals=0),
    )(parity, *arrays)


def program(ensemble, obs_index, obs_value, obs_var):
    bands = lax.axis_size("space")
    tiles = lax.axis_size("member")
    tile = lax.axis_index("member")
    up = [(i, (i + 1) % bands) for i in range(bands)]
    down = [(j, i) for i, j in up]
    sibling_pairs = [(i, i ^ 1) for i in range(tiles)]
    other_pairs = [(i, (i + 1) % tiles if i % 2 else (i - 1) % tiles) for i in range(tiles)]

    near_members = ensemble.shape[1]
    fields, tile = lax.optimization_barrier((ensemble[0].transpose(1, 2, 0, 3), tile))
    parity = (tile % 2).astype(jnp.int32).reshape(1)
    chunks = forecast(fields, up, down)
    region = lax.all_to_all(chunks, "member", 0, 0, tiled=True).reshape(MEMBERS, COLS)
    regions = [region]
    own = region_weights(regions, tile.reshape(1), obs_index[0, 0], obs_value[0, 0], obs_var[0, 0])

    other = lax.ppermute(own, "member", other_pairs)
    below = lax.ppermute(own, "space", up)
    above = lax.ppermute(own, "space", down)
    sibling = lax.ppermute(own, "member", sibling_pairs)
    below_other = lax.ppermute(other, "space", up)
    above_other = lax.ppermute(other, "space", down)
    below_sibling = lax.ppermute(below, "member", sibling_pairs)
    above_sibling = lax.ppermute(above, "member", sibling_pairs)
    total_shape = jax.ShapeDtypeStruct((MEMBERS, COLS), f32)
    dev_shape = jax.ShapeDtypeStruct((MEMBERS, COLS), bf16)
    out_shape = jax.ShapeDtypeStruct((tiles, near_members, COLS), bf16)
    mean_scratch = [pltpu.VMEM((1, COLS), f32)]
    acc, dev = call(own_kernel, (total_shape, dev_shape), 400_000_000, mean_scratch, parity, *regions, own)
    acc = call(near_kernel, total_shape, 1_200_000_000, [], parity, acc, dev, sibling, other, below, above, alias=True)
    acc = call(side_kernel, total_shape, 400_000_000, [], parity, acc, dev, below_sibling, above_sibling, alias=True)
    analysed = call(far_kernel, out_shape, 400_000_000, [], parity, acc, dev, below_other, above_other)
    back = lax.all_to_all(analysed, "member", 0, 0, tiled=True)
    back = back.reshape(tiles, near_members, 2, 3, 2, 64).transpose(1, 3, 2, 4, 0, 5)
    return back.reshape(1, near_members, 3, 4, tiles * 64)


def solution(mesh):
    return jax.shard_map(
        program,
        mesh=mesh,
        in_specs=(
            P("group", "member", None, "space", None),
            P("group", "space", None, None),
            P("group", "space", "member", None),
            P("group", "space", "member", None),
        ),
        out_specs=P("group", "member", None, "space", None),
        check_vma=False,
    )
```

profile of v0, /device:TPU:1, one launch (start us, length us, event | category | flops | bytes accessed | tf_op | source)
XLA Modules:
  0.0 137.0 jit_solution(15070696172265962636)
XLA Ops:
  0.0 1.3 copy.11
  1.3 0.1 slice_bitcast_fusion.1
  1.5 2.2 %collective-permute-start.4 = (bf16[8,32,512]{2,1,0:T(8,128)(2,1)S(1)}, bf16[8,32,512]{2,1,0:T(8,128)(2,1)S(1)}, u32[]{:S(2)}, u32[]{:S(2)}) collective-permute-start(bf16[8,32,512]{2,1,0:T(8,128)(2,1)S(1)} %pad_maximum_fusion.2), channel_id=1, source_target_pairs={{0,2},{2,4},{4,6},{6,8},{8,10},{10,12},{12,14},{14,16},{16,18},{18... | collective-permute-start | bytes 786440 | tf_op jit(solution)/shard_map/ppermute | solution.py:131
  3.7 3.7 %collective-permute-start.5 = (bf16[8,32,512]{2,1,0:T(8,128)(2,1)S(1)}, bf16[8,32,512]{2,1,0:T(8,128)(2,1)S(1)}, u32[]{:S(2)}, u32[]{:S(2)}) collective-permute-start(bf16[8,32,512]{2,1,0:T(8,128)(2,1)S(1)} %pad_maximum_fusion.3), channel_id=1, source_target_pairs={{2,0},{4,2},{6,4},{8,6},{10,8},{12,10},{14,12},{16,14},{18,16},{20... | collective-permute-start | bytes 786440 | tf_op jit(solution)/shard_map/ppermute | solution.py:131
  7.5 1.5 %collective-permute-start.1 = (bf16[8,32,512]{2,1,0:T(8,128)(2,1)S(1)}, bf16[8,32,512]{2,1,0:T(8,128)(2,1)S(1)}, u32[]{:S(2)}, u32[]{:S(2)}) collective-permute-start(bf16[8,32,512]{2,1,0:T(8,128)(2,1)S(1)} %pad_maximum_fusion.1), channel_id=1, source_target_pairs={{2,0},{4,2},{6,4},{8,6},{10,8},{12,10},{14,12},{16,14},{18,16},{20... | collective-permute-start | bytes 786440 | tf_op jit(solution)/shard_map/ppermute | solution.py:131
  9.0 0.1 collective-permute-start
  9.1 0.1 fusion
  9.2 2.3 %collective-permute-done.4.below = bf16[8,32,512]{2,1,0:T(8,128)(2,1)S(1)} collective-permute-done((bf16[8,32,512]{2,1,0:T(8,128)(2,1)S(1)}, bf16[8,32,512]{2,1,0:T(8,128)(2,1)S(1)}, u32[]{:S(2)}, u32[]{:S(2)}) %collective-permute-start.4) | collective-permute-done | bytes 262176 | tf_op jit(solution)/shard_map/ppermute | solution.py:131
  11.5 0.0 collective-permute-done.5.above
  11.5 1.3 shard_map.47
  12.8 0.6 collective-permute-start.6
  13.4 4.3 %collective-permute-start.7 = (bf16[8,32,512]{2,1,0:T(8,128)(2,1)S(1)}, bf16[8,32,512]{2,1,0:T(8,128)(2,1)S(1)}, u32[]{:S(2)}, u32[]{:S(2)}) collective-permute-start(bf16[8,32,512]{2,1,0:T(8,128)(2,1)S(1)} %get-tuple-element.22), channel_id=1, source_target_pairs={{2,0},{4,2},{6,4},{8,6},{10,8},{12,10},{14,12},{16,14},{18,16},{20... | collective-permute-start | bytes 786440 | tf_op jit(solution)/shard_map/ppermute | solution.py:131
  17.6 0.0 collective-permute-done.1.above
  17.6 1.1 collective-permute-done.below
  18.8 1.3 shard_map.46
  20.1 0.1 collective-permute-start.2
  20.1 4.8 %collective-permute-start.3 = (bf16[8,32,512]{2,1,0:T(8,128)(2,1)S(1)}, bf16[8,32,512]{2,1,0:T(8,128)(2,1)S(1)}, u32[]{:S(2)}, u32[]{:S(2)}) collective-permute-start(bf16[8,32,512]{2,1,0:T(8,128)(2,1)S(1)} %get-tuple-element.19), channel_id=1, source_target_pairs={{2,0},{4,2},{6,4},{8,6},{10,8},{12,10},{14,12},{16,14},{18,16},{20... | collective-permute-start | bytes 786440 | tf_op jit(solution)/shard_map/ppermute | solution.py:131
  24.9 0.0 collective-permute-done.6.below
  24.9 0.0 collective-permute-done.7.above
  24.9 1.5 %shard_map.48.refs_0_ = bf16[8,64,768]{2,1,0:T(8,128)(2,1)S(1)} custom-call(f32[3,4,32,512]{3,2,1,0:T(8,128)S(1)} %get-tuple-element.20.now, bf16[8,32,512]{2,1,0:T(8,128)(2,1)S(1)} %collective-permute-done.6.below, bf16[8,32,512]{2,1,0:T(8,128)(2,1)S(1)} %collective-permute-done.7.above), custom_call_target="tpu_custom_call" | custom-call | flops 50000000 | bytes 1000000 | tf_op jit(solution)/shard_map/pallas_call | solution.py:141
  26.4 4.0 %collective-permute-done.2.below = bf16[8,32,512]{2,1,0:T(8,128)(2,1)S(1)} collective-permute-done((bf16[8,32,512]{2,1,0:T(8,128)(2,1)S(1)}, bf16[8,32,512]{2,1,0:T(8,128)(2,1)S(1)}, u32[]{:S(2)}, u32[]{:S(2)}) %collective-permute-start.2) | collective-permute-done | bytes 262176 | tf_op jit(solution)/shard_map/ppermute | solution.py:131
  30.4 0.0 collective-permute-done.3.above
  30.4 0.0 copy-start
  30.4 0.0 copy-start.1
  30.4 0.0 copy-start.2
  30.4 1.5 %shard_map.49 = bf16[8,64,768]{2,1,0:T(8,128)(2,1)S(1)} custom-call(f32[3,4,32,512]{3,2,1,0:T(8,128)S(1)} %get-tuple-element.17.now, bf16[8,32,512]{2,1,0:T(8,128)(2,1)S(1)} %collective-permute-done.2.below, bf16[8,32,512]{2,1,0:T(8,128)(2,1)S(1)} %collective-permute-done.3.above, ...), custom_call_target="tpu_custom_call", output_to_operand_aliasing={{}: (3, {})} | custom-call | flops 50000000 | bytes 1000000 | tf_op jit(solution)/shard_map/pallas_call | solution.py:141
  31.9 31.4 %all_to_all.10 = bf16[8,64,768]{2,1,0:T(8,128)(2,1)S(1)} all-to-all(bf16[8,64,768]{2,1,0:T(8,128)(2,1)S(1)} %shard_map.49), channel_id=1, replica_groups=mesh['member'=8,'space'=16,'group'=2] {'member'}, dimensions={0} | all-to-all | bytes 1572864 | tf_op jit(solution)/shard_map/all_to_all | solution.py:440
  63.3 0.0 copy-done
  63.3 0.0 copy-done.1
  63.3 0.0 copy-done.2
  63.3 6.8 %weights.1.refs_2_ = bf16[1344,128]{1,0:T(8,128)(2,1)} custom-call(bf16[512,768]{1,0:T(8,128)(2,1)S(1)} %bitcast.38, s32[1]{0:T(128)} %bitcast.16.refs_1_, s32[8,256]{1,0:T(8,128)S(1)} %bitcast.40, f32[1,256]{1,0:T(1,128)S(1)} %bitcast.41, f32[1,256]{1,0:T(1,128)S(1)} %bitcast.42), custom_call_target="tpu_custom_call" | custom-call | flops 6000000000 | bytes 1000000 | tf_op jit(solution)/shard_map/weights/pallas_call | solution.py:301
  70.1 0.0 collective-permute-start.10
  70.1 5.1 %collective-permute-start.11 = (bf16[1344,128]{1,0:T(8,128)(2,1)}, bf16[1344,128]{1,0:T(8,128)(2,1)S(1)}, u32[]{:S(2)}, u32[]{:S(2)}) collective-permute-start(bf16[1344,128]{1,0:T(8,128)(2,1)} %weights.1.refs_2_), channel_id=1, source_target_pairs={{2,0},{4,2},{6,4},{8,6},{10,8},{12,10},{14,12},{16,14},{18,16},{20... | collective-permute-start | bytes 1032200 | tf_op jit(solution)/shard_map/ppermute | solution.py:446
  75.1 4.4 %collective-permute-start.9 = (bf16[1344,128]{1,0:T(8,128)(2,1)}, bf16[1344,128]{1,0:T(8,128)(2,1)S(1)}, u32[]{:S(2)}, u32[]{:S(2)}) collective-permute-start(bf16[1344,128]{1,0:T(8,128)(2,1)} %weights.1.refs_2_), channel_id=1, source_target_pairs={{0,224},{32,64},{64,32},{96,128},{128,96},{160,192},{192,160},{224... | collective-permute-start | bytes 1032200 | tf_op jit(solution)/shard_map/ppermute | solution.py:444
  79.5 0.0 collective-permute-start.8
  79.6 0.4 collective-permute-done.10.below
  80.0 4.5 %collective-permute-start.12 = (bf16[1344,128]{1,0:T(8,128)(2,1)S(1)}, bf16[1344,128]{1,0:T(8,128)(2,1)S(1)}, u32[]{:S(2)}, u32[]{:S(2)}) collective-permute-start(bf16[1344,128]{1,0:T(8,128)(2,1)S(1)} %collective-permute-done.10.below), channel_id=1, source_target_pairs={{0,32},{32,0},{64,96},{96,64},{128,160},{160,128},{192,224},{224,1... | collective-permute-start | bytes 1032200 | tf_op jit(solution)/shard_map/ppermute | solution.py:450
  84.5 0.0 collective-permute-done.11.above
  84.5 0.0 collective-permute-start.13
  84.5 4.2 %collective-permute-done.9.other = bf16[1344,128]{1,0:T(8,128)(2,1)S(1)} collective-permute-done((bf16[1344,128]{1,0:T(8,128)(2,1)}, bf16[1344,128]{1,0:T(8,128)(2,1)S(1)}, u32[]{:S(2)}, u32[]{:S(2)}) %collective-permute-start.9) | collective-permute-done | bytes 344096 | tf_op jit(solution)/shard_map/ppermute | solution.py:444
  88.7 0.0 collective-permute-start.14
  88.7 4.8 %collective-permute-start.15 = (bf16[1344,128]{1,0:T(8,128)(2,1)S(1)}, bf16[1344,128]{1,0:T(8,128)(2,1)S(1)}, u32[]{:S(2)}, u32[]{:S(2)}) collective-permute-start(bf16[1344,128]{1,0:T(8,128)(2,1)S(1)} %collective-permute-done.9.other), channel_id=1, source_target_pairs={{2,0},{4,2},{6,4},{8,6},{10,8},{12,10},{14,12},{16,14},{18,16},{20... | collective-permute-start | bytes 1032200 | tf_op jit(solution)/shard_map/ppermute | solution.py:449
  93.5 2.6 %shard_map.50 = (f32[512,768]{1,0:T(8,128)S(1)}, bf16[512,768]{1,0:T(8,128)(2,1)S(1)}) custom-call(s32[1]{0:T(128)} %bitcast.2.refs_0_.parity, bf16[512,768]{1,0:T(8,128)(2,1)S(1)} %bitcast.39, bf16[1344,128]{1,0:T(8,128)(2,1)} %weights.1.refs_2_), custom_call_target="tpu_custom_call" | custom-call | flops 400000000 | bytes 1000000 | tf_op jit(solution)/shard_map/pallas_call | solution.py:415
  96.1 0.0 collective-permute-done.8.sibling
  96.1 5.0 %shard_map.51.acc_in = f32[512,768]{1,0:T(8,128)S(1)} custom-call(s32[1]{0:T(128)} %bitcast.2.refs_0_.parity, f32[512,768]{1,0:T(8,128)S(1)} %get-tuple-element.23.acc_in, bf16[512,768]{1,0:T(8,128)(2,1)S(1)} %get-tuple-element.24.dev, bf16[1344,128]{1,0:T(8,128)(2,1)S(1)} %collective-permute-done.8.sibling, ...), custom_call_target="tpu_custom_call", output_to_operand_aliasing={{}: (1, {})} | custom-call | flops 1200000000 | bytes 1000000 | tf_op jit(solution)/shard_map/pallas_call | solution.py:415
  101.1 0.0 collective-permute-done.12.below_sibling
  101.1 0.0 collective-permute-done.13.above_sibling
  101.1 2.3 %shard_map.52.acc = f32[512,768]{1,0:T(8,128)S(1)} custom-call(s32[1]{0:T(128)} %bitcast.2.refs_0_.parity, f32[512,768]{1,0:T(8,128)S(1)} %shard_map.51.acc_in, bf16[512,768]{1,0:T(8,128)(2,1)S(1)} %get-tuple-element.24.dev, bf16[1344,128]{1,0:T(8,128)(2,1)S(1)} %collective-permute-done.12.below_sibling, ...), custom_call_target="tpu_custom_call", output_to_operand_aliasing={{}: (1, {})} | custom-call | flops 400000000 | bytes 1000000 | tf_op jit(solution)/shard_map/pallas_call | solution.py:415
  103.4 0.0 collective-permute-done.14.below_other
  103.4 0.0 collective-permute-done.15.above_other
  103.4 2.3 %shard_map.53 = bf16[8,64,768]{2,1,0:T(8,128)(2,1)S(1)} custom-call(s32[1]{0:T(128)} %bitcast.2.refs_0_.parity, f32[512,768]{1,0:T(8,128)S(1)} %shard_map.52.acc, bf16[512,768]{1,0:T(8,128)(2,1)S(1)} %get-tuple-element.24.dev, bf16[1344,128]{1,0:T(8,128)(2,1)S(1)} %collective-permute-done.14.below_other, ...), custom_call_target="tpu_custom_call" | custom-call | flops 400000000 | bytes 1000000 | tf_op jit(solution)/shard_map/pallas_call | solution.py:415
  105.7 27.0 %all_to_all.11 = bf16[8,64,768]{2,1,0:T(8,128)(2,1)S(1)} all-to-all(bf16[8,64,768]{2,1,0:T(8,128)(2,1)S(1)} %shard_map.53), channel_id=1, replica_groups=mesh['member'=8,'space'=16,'group'=2] {'member'}, dimensions={0} | all-to-all | bytes 1572864 | tf_op jit(solution)/shard_map/all_to_all | solution.py:460
  132.7 0.9 reshape.18
  133.6 1.8 %copy.9 = bf16[64,3,2,2,8,64]{5,4,3,2,1,0:T(8,128)(2,1)S(1)} copy(bf16[64,3,2,2,8,64]{5,3,1,2,0,4:T(2,128)(2,1)S(1)} %bitcast.46) | data formatting | bytes 1572864 | tf_op jit(solution)/shard_map/transpose | solution.py:461
  135.4 1.6 %reshape.19 = bf16[1,64,3,4,512]{4,3,2,1,0:T(4,128)(2,1)} reshape(bf16[64,3,2,2,8,64]{5,4,3,2,1,0:T(8,128)(2,1)S(1)} %copy.9) | data formatting | bytes 1572864 | tf_op jit(solution)/shard_map/reshape | solution.py:462
  (5 shorter events, 0.2 us)
Async XLA Ops:
  1.5 10.0 %collective-permute-start.4 = (bf16[8,32,512]{2,1,0:T(8,128)(2,1)S(1)}, bf16[8,32,512]{2,1,0:T(8,128)(2,1)S(1)}, u32[]{:S(2)}, u32[]{:S(2)}) collective-permute-start(bf16[8,32,512]{2,1,0:T(8,128)(2,1)S(1)} %pad_maximum_fusion.2), channel_id=1, source_target_pairs={{0,2},{2,4},{4,6},{6,8},{8,10},{10,12},{12,14},{14,16},{16,18},{18... | collective-permute-start | bytes 786440 | tf_op jit(solution)/shard_map/ppermute | solution.py:131
  3.7 7.8 %collective-permute-start.5 = (bf16[8,32,512]{2,1,0:T(8,128)(2,1)S(1)}, bf16[8,32,512]{2,1,0:T(8,128)(2,1)S(1)}, u32[]{:S(2)}, u32[]{:S(2)}) collective-permute-start(bf16[8,32,512]{2,1,0:T(8,128)(2,1)S(1)} %pad_maximum_fusion.3), channel_id=1, source_target_pairs={{2,0},{4,2},{6,4},{8,6},{10,8},{12,10},{14,12},{16,14},{18,16},{20... | collective-permute-start | bytes 786440 | tf_op jit(solution)/shard_map/ppermute | solution.py:131
  7.5 10.2 %collective-permute-start.1 = (bf16[8,32,512]{2,1,0:T(8,128)(2,1)S(1)}, bf16[8,32,512]{2,1,0:T(8,128)(2,1)S(1)}, u32[]{:S(2)}, u32[]{:S(2)}) collective-permute-start(bf16[8,32,512]{2,1,0:T(8,128)(2,1)S(1)} %pad_maximum_fusion.1), channel_id=1, source_target_pairs={{2,0},{4,2},{6,4},{8,6},{10,8},{12,10},{14,12},{16,14},{18,16},{20... | collective-permute-start | bytes 786440 | tf_op jit(solution)/shard_map/ppermute | solution.py:131
  9.0 9.7 %collective-permute-start = (bf16[8,32,512]{2,1,0:T(8,128)(2,1)S(1)}, bf16[8,32,512]{2,1,0:T(8,128)(2,1)S(1)}, u32[]{:S(2)}, u32[]{:S(2)}) collective-permute-start(bf16[8,32,512]{2,1,0:T(8,128)(2,1)S(1)} %pad_maximum_fusion), channel_id=1, source_target_pairs={{0,2},{2,4},{4,6},{6,8},{8,10},{10,12},{12,14},{14,16},{16,18},{18... | collective-permute-start | bytes 786440 | tf_op jit(solution)/shard_map/ppermute | solution.py:131
  12.8 12.2 %collective-permute-start.6 = (bf16[8,32,512]{2,1,0:T(8,128)(2,1)S(1)}, bf16[8,32,512]{2,1,0:T(8,128)(2,1)S(1)}, u32[]{:S(2)}, u32[]{:S(2)}) collective-permute-start(bf16[8,32,512]{2,1,0:T(8,128)(2,1)S(1)} %get-tuple-element.21), channel_id=1, source_target_pairs={{0,2},{2,4},{4,6},{6,8},{8,10},{10,12},{12,14},{14,16},{16,18},{18... | collective-permute-start | bytes 786440 | tf_op jit(solution)/shard_map/ppermute | solution.py:131
  13.4 11.6 %collective-permute-start.7 = (bf16[8,32,512]{2,1,0:T(8,128)(2,1)S(1)}, bf16[8,32,512]{2,1,0:T(8,128)(2,1)S(1)}, u32[]{:S(2)}, u32[]{:S(2)}) collective-permute-start(bf16[8,32,512]{2,1,0:T(8,128)(2,1)S(1)} %get-tuple-element.22), channel_id=1, source_target_pairs={{2,0},{4,2},{6,4},{8,6},{10,8},{12,10},{14,12},{16,14},{18,16},{20... | collective-permute-start | bytes 786440 | tf_op jit(solution)/shard_map/ppermute | solution.py:131
  20.1 10.3 %collective-permute-start.2 = (bf16[8,32,512]{2,1,0:T(8,128)(2,1)S(1)}, bf16[8,32,512]{2,1,0:T(8,128)(2,1)S(1)}, u32[]{:S(2)}, u32[]{:S(2)}) collective-permute-start(bf16[8,32,512]{2,1,0:T(8,128)(2,1)S(1)} %get-tuple-element.18), channel_id=1, source_target_pairs={{0,2},{2,4},{4,6},{6,8},{8,10},{10,12},{12,14},{14,16},{16,18},{18... | collective-permute-start | bytes 786440 | tf_op jit(solution)/shard_map/ppermute | solution.py:131
  20.1 10.3 %collective-permute-start.3 = (bf16[8,32,512]{2,1,0:T(8,128)(2,1)S(1)}, bf16[8,32,512]{2,1,0:T(8,128)(2,1)S(1)}, u32[]{:S(2)}, u32[]{:S(2)}) collective-permute-start(bf16[8,32,512]{2,1,0:T(8,128)(2,1)S(1)} %get-tuple-element.19), channel_id=1, source_target_pairs={{2,0},{4,2},{6,4},{8,6},{10,8},{12,10},{14,12},{16,14},{18,16},{20... | collective-permute-start | bytes 786440 | tf_op jit(solution)/shard_map/ppermute | solution.py:131
  30.4 32.9 %copy-start = (s32[1,1,8,256]{3,2,1,0:T(8,128)S(1)}, s32[1,1,8,256]{3,2,1,0:T(8,128)}, u32[]{:S(2)}) copy-start(s32[1,1,8,256]{3,2,1,0:T(8,128)} %param.5) | copy-start | bytes 24580
  30.4 32.9 %copy-start.1 = (f32[1,1,1,256]{3,2,1,0:T(1,128)S(1)}, f32[1,1,1,256]{3,2,1,0:T(1,128)}, u32[]{:S(2)}) copy-start(f32[1,1,1,256]{3,2,1,0:T(1,128)} %param.6) | copy-start | bytes 3076
  30.4 32.9 %copy-start.2 = (f32[1,1,1,256]{3,2,1,0:T(1,128)S(1)}, f32[1,1,1,256]{3,2,1,0:T(1,128)}, u32[]{:S(2)}) copy-start(f32[1,1,1,256]{3,2,1,0:T(1,128)} %param.7) | copy-start | bytes 3076
  70.1 9.9 %collective-permute-start.10 = (bf16[1344,128]{1,0:T(8,128)(2,1)}, bf16[1344,128]{1,0:T(8,128)(2,1)S(1)}, u32[]{:S(2)}, u32[]{:S(2)}) collective-permute-start(bf16[1344,128]{1,0:T(8,128)(2,1)} %weights.1.refs_2_), channel_id=1, source_target_pairs={{0,2},{2,4},{4,6},{6,8},{8,10},{10,12},{12,14},{14,16},{16,18},{18... | collective-permute-start | bytes 1032200 | tf_op jit(solution)/shard_map/ppermute | solution.py:445
  70.1 14.4 %collective-permute-start.11 = (bf16[1344,128]{1,0:T(8,128)(2,1)}, bf16[1344,128]{1,0:T(8,128)(2,1)S(1)}, u32[]{:S(2)}, u32[]{:S(2)}) collective-permute-start(bf16[1344,128]{1,0:T(8,128)(2,1)} %weights.1.refs_2_), channel_id=1, source_target_pairs={{2,0},{4,2},{6,4},{8,6},{10,8},{12,10},{14,12},{16,14},{18,16},{20... | collective-permute-start | bytes 1032200 | tf_op jit(solution)/shard_map/ppermute | solution.py:446
  75.1 13.6 %collective-permute-start.9 = (bf16[1344,128]{1,0:T(8,128)(2,1)}, bf16[1344,128]{1,0:T(8,128)(2,1)S(1)}, u32[]{:S(2)}, u32[]{:S(2)}) collective-permute-start(bf16[1344,128]{1,0:T(8,128)(2,1)} %weights.1.refs_2_), channel_id=1, source_target_pairs={{0,224},{32,64},{64,32},{96,128},{128,96},{160,192},{192,160},{224... | collective-permute-start | bytes 1032200 | tf_op jit(solution)/shard_map/ppermute | solution.py:444
  79.5 16.6 %collective-permute-start.8 = (bf16[1344,128]{1,0:T(8,128)(2,1)}, bf16[1344,128]{1,0:T(8,128)(2,1)S(1)}, u32[]{:S(2)}, u32[]{:S(2)}) collective-permute-start(bf16[1344,128]{1,0:T(8,128)(2,1)} %weights.1.refs_2_), channel_id=1, source_target_pairs={{0,32},{32,0},{64,96},{96,64},{128,160},{160,128},{192,224},{224,1... | collective-permute-start | bytes 1032200 | tf_op jit(solution)/shard_map/ppermute | solution.py:447
  80.0 21.1 %collective-permute-start.12 = (bf16[1344,128]{1,0:T(8,128)(2,1)S(1)}, bf16[1344,128]{1,0:T(8,128)(2,1)S(1)}, u32[]{:S(2)}, u32[]{:S(2)}) collective-permute-start(bf16[1344,128]{1,0:T(8,128)(2,1)S(1)} %collective-permute-done.10.below), channel_id=1, source_target_pairs={{0,32},{32,0},{64,96},{96,64},{128,160},{160,128},{192,224},{224,1... | collective-permute-start | bytes 1032200 | tf_op jit(solution)/shard_map/ppermute | solution.py:450
  84.5 16.6 %collective-permute-start.13 = (bf16[1344,128]{1,0:T(8,128)(2,1)S(1)}, bf16[1344,128]{1,0:T(8,128)(2,1)S(1)}, u32[]{:S(2)}, u32[]{:S(2)}) collective-permute-start(bf16[1344,128]{1,0:T(8,128)(2,1)S(1)} %collective-permute-done.11.above), channel_id=1, source_target_pairs={{0,32},{32,0},{64,96},{96,64},{128,160},{160,128},{192,224},{224,1... | collective-permute-start | bytes 1032200 | tf_op jit(solution)/shard_map/ppermute | solution.py:451
  88.7 14.7 %collective-permute-start.14 = (bf16[1344,128]{1,0:T(8,128)(2,1)S(1)}, bf16[1344,128]{1,0:T(8,128)(2,1)S(1)}, u32[]{:S(2)}, u32[]{:S(2)}) collective-permute-start(bf16[1344,128]{1,0:T(8,128)(2,1)S(1)} %collective-permute-done.9.other), channel_id=1, source_target_pairs={{0,2},{2,4},{4,6},{6,8},{8,10},{10,12},{12,14},{14,16},{16,18},{18... | collective-permute-start | bytes 1032200 | tf_op jit(solution)/shard_map/ppermute | solution.py:448
  88.7 14.7 %collective-permute-start.15 = (bf16[1344,128]{1,0:T(8,128)(2,1)S(1)}, bf16[1344,128]{1,0:T(8,128)(2,1)S(1)}, u32[]{:S(2)}, u32[]{:S(2)}) collective-permute-start(bf16[1344,128]{1,0:T(8,128)(2,1)S(1)} %collective-permute-done.9.other), channel_id=1, source_target_pairs={{2,0},{4,2},{6,4},{8,6},{10,8},{12,10},{14,12},{16,14},{18,16},{20... | collective-permute-start | bytes 1032200 | tf_op jit(solution)/shard_map/ppermute | solution.py:449
where the time goes:
time: 137 us
  blocking collectives  58.4 us (43%)
  starting transfers between devices  36.1 us (26%)
  Pallas kernels  24.4 us (18%)
  waiting for transfers between devices  12 us (9%)
  local copies, waits for them, and re-layouts  5.77 us (4%)
    all_to_all x1, blocking collectives, program(): lax.all_to_all(chunks, 'member', 0, 0, tiled=True).reshape(MEMBERS, COLS)  31.4 us
    all_to_all x1, blocking collectives, program(): back = lax.all_to_all(analysed, 'member', 0, 0, tiled=True)  27 us
    ppermute x8, starting transfers between devices, swapped(): return (lax.ppermute(last, 'space', up), lax.ppermute(first, 'space', down))  17.3 us
    pallas_call x4, Pallas kernels, call(): pl.pallas_call(kernel, out_shape=outs, in_specs=[smem] + [vmem] * len(arr...  12.1 us
    ppermute x8, waiting for transfers between devices, swapped(): return (lax.ppermute(last, 'space', up), lax.ppermute(first, 'space', down))  7.41 us
    pallas_call x1, Pallas kernels, region_weights(): pl.pallas_call(weights_kernel, out_shape=jax.ShapeDtypeStruct((PACKED, BL...  6.8 us
    pallas_call x4, Pallas kernels, step(): pl.pallas_call(kernel, out_shape=outs, in_specs=[vmem] * len(arrays), out...  5.54 us
    ppermute x1, starting transfers between devices, program(): above = lax.ppermute(own, 'space', down)  5.06 us
  transfers between devices with their start and end apart: 16, of which 5 were waited for; matrix products, arithmetic and copies ran while one was open for 0% of the time, Pallas kernels for 10%

commit v1 on v0

--- a/solution.py
+++ b/solution.py
@@ -15,6 +15,7 @@
 BLOCK = 128
 PAIRS = [(i, j) for i in range(4) for j in range(i, 4)]
 CENTRE_AT = len(PAIRS) * BLOCK
+FRONT = len(PAIRS) // 2 * BLOCK
 PACKED = CENTRE_AT + 4 * 16
 
 time_step = 0.4
@@ -199,8 +200,16 @@
 
 def weights_kernel(*refs):
     regions = refs[:HALVES]
-    tile, index, value, var, packed = refs[HALVES : HALVES + 5]
-    z_ref, zt_ref, b_ref, m_ref, l_ref, u_ref = refs[HALVES + 5 :]
+    tile, index, value, var, packed, front, back = refs[HALVES : HALVES + 7]
+    z_ref, zt_ref, b_ref, m_ref, l_ref, u_ref = refs[HALVES + 7 :]
+
+    def put(start, rows):
+        packed[start : start + rows.shape[0], :] = rows
+        if start < FRONT:
+            front[start : start + rows.shape[0], :] = rows
+        else:
+            back[start - FRONT : start - FRONT + rows.shape[0], :] = rows
+
     identity = eye(OBS)
 
     def as_column(row):
@@ -288,21 +297,22 @@
             block = band[:, (j - i) * BLOCK : (j - i + 1) * BLOCK]
             if i == j:
                 block = block + (scale * low) * small
-            packed[at : at + BLOCK, :] = block.astype(bf16)
+            put(at, block.astype(bf16))
             at += BLOCK
         piece = centre[:, i * BLOCK : (i + 1) * BLOCK]
         high = piece.astype(bf16).astype(f32)
         both = jnp.where(spot == 0, high, jnp.where(spot == 1, piece - high, 0.0))
-        start = CENTRE_AT + 16 * i
-        packed[start : start + 16, :] = both.astype(bf16)
+        put(CENTRE_AT + 16 * i, both.astype(bf16))
 
 
 def region_weights(regions, tile, index, values, variances):
     return pl.pallas_call(
         weights_kernel,
-        out_shape=jax.ShapeDtypeStruct((PACKED, BLOCK), bf16),
+        out_shape=[
+            jax.ShapeDtypeStruct((size, BLOCK), bf16) for size in (PACKED, FRONT, PACKED - FRONT)
+        ],
         in_specs=[vmem] * HALVES + [smem] + [vmem] * 3,
-        out_specs=pl.BlockSpec(memory_space=pltpu.VMEM),
+        out_specs=[vmem] * 3,
         scratch_shapes=[
             pltpu.VMEM((MEMBERS, OBS), f32),
             pltpu.VMEM((OBS, MEMBERS), f32),
@@ -340,40 +350,40 @@
     return {(row, s): (r if row else 1.0 - r) * side[s] for row in (0, 1) for s in (0, 1, 2)}
 
 
-def unpack(source, base, full):
+def piece(source, start, size):
+    if not isinstance(source, tuple):
+        return source[start : start + size, :]
+    if start < FRONT:
+        return source[0][start : start + size, :]
+    return source[1][start - FRONT : start - FRONT + size, :]
+
+
+def unpack(source, full):
     for n, (i, j) in enumerate(PAIRS):
-        block = source[base + n * BLOCK : base + (n + 1) * BLOCK, :]
+        block = piece(source, n * BLOCK, BLOCK)
         full[i * BLOCK : (i + 1) * BLOCK, j * BLOCK : (j + 1) * BLOCK] = block
         if i != j:
-            turned = jnp.transpose(block.astype(f32)).astype(bf16)
+            turned = jnp.transpose(block)
             full[j * BLOCK : (j + 1) * BLOCK, i * BLOCK : (i + 1) * BLOCK] = turned
 
 
-def apply(source, base, full, dev, acc, lo, hi, factor, before=None, out=None):
-    unpack(source, base, full)
-    shift = jnp.zeros((16, hi - lo), f32)
+def apply(source, full, dev, acc, lo, hi, factor, before=None, out=None):
+    unpack(source, full)
     for i in range(4):
-        start = base + CENTRE_AT + 16 * i
-        shift = shift + dot(source[start : start + 16, :], dev[i * BLOCK : (i + 1) * BLOCK, lo:hi])
-    shift = jnp.sum(shift, axis=0, keepdims=True)
-    factor = factor[:, lo:hi]
-    wide = MEMBERS // HALVES // BLOCK
-    slots = BLOCK * 8 // (MEMBERS // HALVES)
-    size = BLOCK // slots
-
-    def rows(i, carry):
-        at = pl.ds(pl.multiple_of(i * BLOCK, BLOCK), BLOCK)
-        term = factor * (dot(full[at, :], dev[:, lo:hi]) + shift)
-        term = term + (acc[at, lo:hi] if before is None else before[:, lo:hi])
+        full[MEMBERS:, i * BLOCK : (i + 1) * BLOCK] = piece(source, CENTRE_AT + 16 * i, 16)
+
+    def part(at):
+        both = dot(full[...], dev[:, at])
+        shift = jnp.sum(both[MEMBERS:], axis=0, keepdims=True)
+        term = factor[:, at] * (both[:MEMBERS] + shift)
+        term = term + (acc[:, at] if before is None else before[:, at])
         if out is None:
-            acc[at, lo:hi] = term
+            acc[:, at] = term
         else:
-            tiles = pl.ds((i % wide) * slots, slots)
-            spot = pl.ds(pl.multiple_of((i // wide) * size, size), size)
-            out[tiles, spot, lo:hi] = term.astype(bf16).reshape(slots, size, hi - lo)
-        return carry
-
-    lax.fori_loop(0, 4, rows, 0)
+            out[:, :, at] = term.astype(bf16).reshape(out.shape[0], out.shape[1], HALF)
+
+    for at in range(lo, hi, HALF):
+        part(slice(at, at + HALF))
 
 
 def own_kernel(*refs):
@@ -388,27 +398,31 @@
         mean_ref[:, at] = mean
         for n, part in enumerate(parts):
             dev[n * size : (n + 1) * size, at] = (part - mean).astype(bf16)
-    apply(own, 0, full, dev, acc, 0, COLS, factors(parity[0])[0, 0], before=mean_ref)
-
-
-def near_kernel(parity, acc_in, dev, sibling, other, below, above, acc, full):
+    apply(own, full, dev, acc, 0, COLS, factors(parity[0])[0, 0], before=mean_ref)
+
+
+def near_kernel(
+    parity, acc_in, dev, sibling, other_front, other_back, below, above, acc, full
+):
     factor = factors(parity[0])
-    apply(sibling, 0, full, dev, acc, 0, COLS, factor[0, 1])
-    apply(other, 0, full, dev, acc, 0, COLS, factor[0, 2])
-    apply(below, 0, full, dev, acc, 0, HALF, factor[1, 0])
-    apply(above, 0, full, dev, acc, HALF, COLS, factor[1, 0])
+    apply(sibling, full, dev, acc, 0, COLS, factor[0, 1])
+    apply((other_front, other_back), full, dev, acc, 0, COLS, factor[0, 2])
+    apply(below, full, dev, acc, 0, HALF, factor[1, 0])
+    apply(above, full, dev, acc, HALF, COLS, factor[1, 0])
 
 
 def side_kernel(parity, acc_in, dev, below_sibling, above_sibling, acc, full):
     factor = factors(parity[0])
-    apply(below_sibling, 0, full, dev, acc, 0, HALF, factor[1, 1])
-    apply(above_sibling, 0, full, dev, acc, HALF, COLS, factor[1, 1])
-
-
-def far_kernel(parity, acc, dev, below_other, above_other, out, full):
+    apply(below_sibling, full, dev, acc, 0, HALF, factor[1, 1])
+    apply(above_sibling, full, dev, acc, HALF, COLS, factor[1, 1])
+
+
+def far_kernel(
+    parity, acc, dev, below_front, below_back, above_front, above_back, out, full
+):
     factor = factors(parity[0])
-    apply(below_other, 0, full, dev, acc, 0, HALF, factor[1, 2], out=out)
-    apply(above_other, 0, full, dev, acc, HALF, COLS, factor[1, 2], out=out)
+    apply((below_front, below_back), full, dev, acc, 0, HALF, factor[1, 2], out=out)
+    apply((above_front, above_back), full, dev, acc, HALF, COLS, factor[1, 2], out=out)
 
 
 def call(kernel, outs, flops, scratch, parity, *arrays, alias=False):
@@ -417,11 +431,49 @@
     out_shape=outs,
     in_specs=[smem] + [vmem] * len(arrays),
     out_specs=jax.tree.map(lambda _: vmem, outs),
-    scratch_shapes=[pltpu.VMEM((MEMBERS, MEMBERS), bf16)] + scratch,
+    scratch_shapes=[pltpu.VMEM((MEMBERS + 16, MEMBERS), bf16)] + scratch,
     input_output_aliases={1: 0} if alias else {},
     compiler_params=pltpu.CompilerParams(vmem_limit_bytes=16 * 1024 * 1024),
     cost_estimate=pl.CostEstimate(flops=flops, bytes_accessed=1_000_000, transcendentals=0),
     )(parity, *arrays)
+
+
+def restore_kernel(back, out, held):
+    low = lax.broadcasted_iota(jnp.int32, (GROUP, BLOCK), 1) < 64
+
+    def group(g, carry):
+        at = pl.ds(pl.multiple_of(g * GROUP, GROUP), GROUP)
+        for f in range(3):
+            for p in range(2):
+                place = p * HALF + f * BLOCK
+                for t in range(4):
+                    x = back[2 * t, at, place : place + BLOCK].astype(f32)
+                    y = back[2 * t + 1, at, place : place + BLOCK].astype(f32)
+                    first = jnp.where(low, x, pltpu.roll(y, 64, 1))
+                    second = jnp.where(low, pltpu.roll(x, 64, 1), y)
+                    held[t, pl.ds(2 * p, GROUP, stride=4), :] = first
+                    held[t, pl.ds(2 * p + 1, GROUP, stride=4), :] = second
+            for t in range(4):
+                rows = held[t, :, :].reshape(GROUP, 4, BLOCK)
+                out[0, at, f, :, t * BLOCK : (t + 1) * BLOCK] = rows.astype(bf16)
+        return carry
+
+    lax.fori_loop(0, back.shape[1] // GROUP, group, 0)
+
+
+def restored(back):
+    tiles, members, _ = back.shape
+    columns = tiles * 64
+    return pl.pallas_call(
+        restore_kernel,
+        out_shape=jax.ShapeDtypeStruct((1, members, 3, 4, columns), bf16),
+        in_specs=[vmem],
+        out_specs=vmem,
+        scratch_shapes=[pltpu.VMEM((4, GROUP * 4, BLOCK), f32)],
+        compiler_params=pltpu.CompilerParams(vmem_limit_bytes=12 * 1024 * 1024),
+        cost_estimate=pl.CostEstimate(flops=10_000_000, bytes_accessed=1_000_000, transcendentals=0),
+        name="restore",
+    )(back)
 
 
 def program(ensemble, obs_index, obs_value, obs_var):
@@ -439,14 +491,17 @@
     chunks = forecast(fields, up, down)
     region = lax.all_to_all(chunks, "member", 0, 0, tiled=True).reshape(MEMBERS, COLS)
     regions = [region]
-    own = region_weights(regions, tile.reshape(1), obs_index[0, 0], obs_value[0, 0], obs_var[0, 0])
-
-    other = lax.ppermute(own, "member", other_pairs)
+    own, front, behind = region_weights(regions, tile.reshape(1), obs_index[0, 0], obs_value[0, 0], obs_var[0, 0])
+
+    other_front = lax.ppermute(front, "member", other_pairs)
+    other_back = lax.ppermute(behind, "member", other_pairs)
     below = lax.ppermute(own, "space", up)
     above = lax.ppermute(own, "space", down)
     sibling = lax.ppermute(own, "member", sibling_pairs)
-    below_other = lax.ppermute(other, "space", up)
-    above_other = lax.ppermute(other, "space", down)
+    below_front = lax.ppermute(other_front, "space", up)
+    above_front = lax.ppermute(other_front, "space", down)
+    below_back = lax.ppermute(other_back, "space", up)
+    above_back = lax.ppermute(other_back, "space", down)
     below_sibling = lax.ppermute(below, "member", sibling_pairs)
     above_sibling = lax.ppermute(above, "member", sibling_pairs)
     total_shape = jax.ShapeDtypeStruct((MEMBERS, COLS), f32)
@@ -454,12 +509,11 @@
     out_shape = jax.ShapeDtypeStruct((tiles, near_members, COLS), bf16)
     mean_scratch = [pltpu.VMEM((1, COLS), f32)]
     acc, dev = call(own_kernel, (total_shape, dev_shape), 400_000_000, mean_scratch, parity, *regions, own)
-    acc = call(near_kernel, total_shape, 1_200_000_000, [], parity, acc, dev, sibling, other, below, above, alias=True)
+    acc = call(near_kernel, total_shape, 1_200_000_000, [], parity, acc, dev, sibling, other_front, other_back, below, above, alias=True)
     acc = call(side_kernel, total_shape, 400_000_000, [], parity, acc, dev, below_sibling, above_sibling, alias=True)
-    analysed = call(far_kernel, out_shape, 400_000_000, [], parity, acc, dev, below_other, above_other)
+    analysed = call(far_kernel, out_shape, 400_000_000, [], parity, acc, dev, below_front, below_back, above_front, above_back)
     back = lax.all_to_all(analysed, "member", 0, 0, tiled=True)
-    back = back.reshape(tiles, near_members, 2, 3, 2, 64).transpose(1, 3, 2, 4, 0, 5)
-    return back.reshape(1, near_members, 3, 4, tiles * 64)
+    return restored(back)
 
 
 def solution(mesh):

time: 137 us -> 141 us (1.029)
  starting transfers between devices: 36.1 us -> 44.1 us
  Pallas kernels: 24.4 us -> 19.4 us
  waiting for transfers between devices: 12 us -> 16.9 us
  local copies, waits for them, and re-layouts: 5.77 us -> 1.45 us
    pallas_call x4, Pallas kernels: 12.1 us -> 6.24 us  [call(): pl.pallas_call(kernel, out_shape=outs, in_specs=[smem] + [vmem] * len(arr...]
    ppermute x3 -> x6, waiting for transfers between devices: 4.19 us -> 8.91 us  [the longest x1 8.89 us: program(): other_front = lax.ppermute(front, 'member', other_pairs)]
    ppermute x1, starting transfers between devices: 0.01 us -> 3.94 us  [program(): sibling = lax.ppermute(own, 'member', sibling_pairs)]
    ppermute x3 -> x6, starting transfers between devices: 9.2 us -> 13.1 us  [the longest x1 4.78 us: program(): above_front = lax.ppermute(other_front, 'space', down)]
    reshape x2 -> x0, local copies, waits for them, and re-layouts: 2.49 us -> none  [the longest x1 1.62 us: program(): return back.reshape(1, near_members, 3, 4, tiles * 64)]
    transpose x1 -> x0, local copies, waits for them, and re-layouts: 1.83 us -> none  [program(): back.reshape(tiles, near_members, 2, 3, 2, 64).transpose(1, 3, 2, 4, 0, 5)]
    pallas_call x1 -> x2, Pallas kernels: 6.8 us -> 7.63 us  [the longest x1 6.06 us: region_weights(): pl.pallas_call(weights_kernel, out_shape=[jax.ShapeDtypeStruct((size, BLO...]
  transfers between devices with their start and end apart: 16 -> 19, of which waited for: 5 -> 5; matrix products, arithmetic and copies ran while one was open for 0% -> 0% of each run, Pallas kernels for 10% -> 7%
where the time goes in v1:
time: 141 us
  blocking collectives  58.6 us (42%)
  starting transfers between devices  44.1 us (31%)
  Pallas kernels  19.4 us (14%)
  waiting for transfers between devices  16.9 us (12%)
  local copies, waits for them, and re-layouts  1.45 us (1%)
    all_to_all x1, blocking collectives, program(): lax.all_to_all(chunks, 'member', 0, 0, tiled=True).reshape(MEMBERS, COLS)  31.4 us
    all_to_all x1, blocking collectives, program(): back = lax.all_to_all(analysed, 'member', 0, 0, tiled=True)  27.3 us
    ppermute x8, starting transfers between devices, swapped(): return (lax.ppermute(last, 'space', up), lax.ppermute(first, 'space', down))  17.3 us
    ppermute x1, waiting for transfers between devices, program(): other_front = lax.ppermute(front, 'member', other_pairs)  8.89 us
    ppermute x8, waiting for transfers between devices, swapped(): return (lax.ppermute(last, 'space', up), lax.ppermute(first, 'space', down))  7.41 us
    pallas_call x4, Pallas kernels, call(): pl.pallas_call(kernel, out_shape=outs, in_specs=[smem] + [vmem] * len(arr...  6.24 us
    pallas_call x1, Pallas kernels, region_weights(): pl.pallas_call(weights_kernel, out_shape=[jax.ShapeDtypeStruct((size, BLO...  6.06 us
    pallas_call x4, Pallas kernels, step(): pl.pallas_call(kernel, out_shape=outs, in_specs=[vmem] * len(arrays), out...  5.54 us
  transfers between devices with their start and end apart: 19, of which 5 were waited for; matrix products, arithmetic and copies ran while one was open for 0% of the time, Pallas kernels for 7%

profile of v1, /device:TPU:1, one launch (start us, length us, event | category | flops | bytes accessed | tf_op | source)
XLA Modules:
  0.0 140.8 jit_solution(14179880975840556386)
XLA Ops:
  0.0 1.3 copy.10
  1.3 0.1 slice_bitcast_fusion.1
  1.5 2.2 %collective-permute-start.4 = (bf16[8,32,512]{2,1,0:T(8,128)(2,1)S(1)}, bf16[8,32,512]{2,1,0:T(8,128)(2,1)S(1)}, u32[]{:S(2)}, u32[]{:S(2)}) collective-permute-start(bf16[8,32,512]{2,1,0:T(8,128)(2,1)S(1)} %pad_maximum_fusion.2), channel_id=1, source_target_pairs={{0,2},{2,4},{4,6},{6,8},{8,10},{10,12},{12,14},{14,16},{16,18},{18... | collective-permute-start | bytes 786440 | tf_op jit(solution)/shard_map/ppermute | solution.py:132
  3.7 3.7 %collective-permute-start.5 = (bf16[8,32,512]{2,1,0:T(8,128)(2,1)S(1)}, bf16[8,32,512]{2,1,0:T(8,128)(2,1)S(1)}, u32[]{:S(2)}, u32[]{:S(2)}) collective-permute-start(bf16[8,32,512]{2,1,0:T(8,128)(2,1)S(1)} %pad_maximum_fusion.3), channel_id=1, source_target_pairs={{2,0},{4,2},{6,4},{8,6},{10,8},{12,10},{14,12},{16,14},{18,16},{20... | collective-permute-start | bytes 786440 | tf_op jit(solution)/shard_map/ppermute | solution.py:132
  7.5 1.5 %collective-permute-start.1 = (bf16[8,32,512]{2,1,0:T(8,128)(2,1)S(1)}, bf16[8,32,512]{2,1,0:T(8,128)(2,1)S(1)}, u32[]{:S(2)}, u32[]{:S(2)}) collective-permute-start(bf16[8,32,512]{2,1,0:T(8,128)(2,1)S(1)} %pad_maximum_fusion.1), channel_id=1, source_target_pairs={{2,0},{4,2},{6,4},{8,6},{10,8},{12,10},{14,12},{16,14},{18,16},{20... | collective-permute-start | bytes 786440 | tf_op jit(solution)/shard_map/ppermute | solution.py:132
  9.0 0.1 collective-permute-start
  9.1 0.1 fusion
  9.2 2.3 %collective-permute-done.4.below = bf16[8,32,512]{2,1,0:T(8,128)(2,1)S(1)} collective-permute-done((bf16[8,32,512]{2,1,0:T(8,128)(2,1)S(1)}, bf16[8,32,512]{2,1,0:T(8,128)(2,1)S(1)}, u32[]{:S(2)}, u32[]{:S(2)}) %collective-permute-start.4) | collective-permute-done | bytes 262176 | tf_op jit(solution)/shard_map/ppermute | solution.py:132
  11.5 0.0 collective-permute-done.5.above
  11.5 1.3 shard_map.47
  12.8 0.6 collective-permute-start.6
  13.4 4.3 %collective-permute-start.7 = (bf16[8,32,512]{2,1,0:T(8,128)(2,1)S(1)}, bf16[8,32,512]{2,1,0:T(8,128)(2,1)S(1)}, u32[]{:S(2)}, u32[]{:S(2)}) collective-permute-start(bf16[8,32,512]{2,1,0:T(8,128)(2,1)S(1)} %get-tuple-element.25), channel_id=1, source_target_pairs={{2,0},{4,2},{6,4},{8,6},{10,8},{12,10},{14,12},{16,14},{18,16},{20... | collective-permute-start | bytes 786440 | tf_op jit(solution)/shard_map/ppermute | solution.py:132
  17.6 0.0 collective-permute-done.1.above
  17.6 1.1 collective-permute-done.below
  18.8 1.3 shard_map.46
  20.1 0.1 collective-permute-start.2
  20.1 4.8 %collective-permute-start.3 = (bf16[8,32,512]{2,1,0:T(8,128)(2,1)S(1)}, bf16[8,32,512]{2,1,0:T(8,128)(2,1)S(1)}, u32[]{:S(2)}, u32[]{:S(2)}) collective-permute-start(bf16[8,32,512]{2,1,0:T(8,128)(2,1)S(1)} %get-tuple-element.22), channel_id=1, source_target_pairs={{2,0},{4,2},{6,4},{8,6},{10,8},{12,10},{14,12},{16,14},{18,16},{20... | collective-permute-start | bytes 786440 | tf_op jit(solution)/shard_map/ppermute | solution.py:132
  24.9 0.0 collective-permute-done.6.below
  24.9 0.0 collective-permute-done.7.above
  24.9 1.5 %shard_map.48.refs_0_ = bf16[8,64,768]{2,1,0:T(8,128)(2,1)S(1)} custom-call(f32[3,4,32,512]{3,2,1,0:T(8,128)S(1)} %get-tuple-element.23.now, bf16[8,32,512]{2,1,0:T(8,128)(2,1)S(1)} %collective-permute-done.6.below, bf16[8,32,512]{2,1,0:T(8,128)(2,1)S(1)} %collective-permute-done.7.above), custom_call_target="tpu_custom_call" | custom-call | flops 50000000 | bytes 1000000 | tf_op jit(solution)/shard_map/pallas_call | solution.py:142
  26.4 4.0 %collective-permute-done.2.below = bf16[8,32,512]{2,1,0:T(8,128)(2,1)S(1)} collective-permute-done((bf16[8,32,512]{2,1,0:T(8,128)(2,1)S(1)}, bf16[8,32,512]{2,1,0:T(8,128)(2,1)S(1)}, u32[]{:S(2)}, u32[]{:S(2)}) %collective-permute-start.2) | collective-permute-done | bytes 262176 | tf_op jit(solution)/shard_map/ppermute | solution.py:132
  30.4 0.0 collective-permute-done.3.above
  30.4 0.0 copy-start
  30.4 0.0 copy-start.1
  30.4 0.0 copy-start.2
  30.4 1.5 %shard_map.49 = bf16[8,64,768]{2,1,0:T(8,128)(2,1)S(1)} custom-call(f32[3,4,32,512]{3,2,1,0:T(8,128)S(1)} %get-tuple-element.20.now, bf16[8,32,512]{2,1,0:T(8,128)(2,1)S(1)} %collective-permute-done.2.below, bf16[8,32,512]{2,1,0:T(8,128)(2,1)S(1)} %collective-permute-done.3.above, ...), custom_call_target="tpu_custom_call", output_to_operand_aliasing={{}: (3, {})} | custom-call | flops 50000000 | bytes 1000000 | tf_op jit(solution)/shard_map/pallas_call | solution.py:142
  31.9 31.4 %all_to_all.10 = bf16[8,64,768]{2,1,0:T(8,128)(2,1)S(1)} all-to-all(bf16[8,64,768]{2,1,0:T(8,128)(2,1)S(1)} %shard_map.49), channel_id=1, replica_groups=mesh['member'=8,'space'=16,'group'=2] {'member'}, dimensions={0} | all-to-all | bytes 1572864 | tf_op jit(solution)/shard_map/all_to_all | solution.py:492
  63.3 0.0 copy-done
  63.3 0.0 copy-done.1
  63.3 0.0 copy-done.2
  63.3 6.1 %weights.1 = (bf16[1344,128]{1,0:T(8,128)(2,1)S(1)}, bf16[640,128]{1,0:T(8,128)(2,1)S(1)}, bf16[704,128]{1,0:T(8,128)(2,1)S(1)}) custom-call(bf16[512,768]{1,0:T(8,128)(2,1)S(1)} %bitcast.35, s32[1]{0:T(128)} %bitcast.16.refs_1_, s32[8,256]{1,0:T(8,128)S(1)} %bitcast.37, f32[1,256]{1,0:T(1,128)S(1)} %bitcast.38, f32[1,256]{1,0:T(1,128)S(1)} %bitcast.39), custom_call_target="tpu_custom_call" | custom-call | flops 6000000000 | bytes 1000000 | tf_op jit(solution)/shard_map/weights/pallas_call | solution.py:309
  69.3 0.1 collective-permute-start.11
  69.4 5.1 %collective-permute-start.12 = (bf16[1344,128]{1,0:T(8,128)(2,1)S(1)}, bf16[1344,128]{1,0:T(8,128)(2,1)S(1)}, u32[]{:S(2)}, u32[]{:S(2)}) collective-permute-start(bf16[1344,128]{1,0:T(8,128)(2,1)S(1)} %get-tuple-element.26.refs_2_), channel_id=1, source_target_pairs={{2,0},{4,2},{6,4},{8,6},{10,8},{12,10},{14,12},{16,14},{18,16},{20... | collective-permute-start | bytes 1032200 | tf_op jit(solution)/shard_map/ppermute | solution.py:499
  74.6 3.9 %collective-permute-start.8 = (bf16[1344,128]{1,0:T(8,128)(2,1)S(1)}, bf16[1344,128]{1,0:T(8,128)(2,1)S(1)}, u32[]{:S(2)}, u32[]{:S(2)}) collective-permute-start(bf16[1344,128]{1,0:T(8,128)(2,1)S(1)} %get-tuple-element.26.refs_2_), channel_id=1, source_target_pairs={{0,32},{32,0},{64,96},{96,64},{128,160},{160,128},{192,224},{224,1... | collective-permute-start | bytes 1032200 | tf_op jit(solution)/shard_map/ppermute | solution.py:500
  78.5 0.6 collective-permute-done.11.below
  79.1 4.5 %collective-permute-start.13 = (bf16[1344,128]{1,0:T(8,128)(2,1)S(1)}, bf16[1344,128]{1,0:T(8,128)(2,1)S(1)}, u32[]{:S(2)}, u32[]{:S(2)}) collective-permute-start(bf16[1344,128]{1,0:T(8,128)(2,1)S(1)} %collective-permute-done.11.below), channel_id=1, source_target_pairs={{0,32},{32,0},{64,96},{96,64},{128,160},{160,128},{192,224},{224,1... | collective-permute-start | bytes 1032200 | tf_op jit(solution)/shard_map/ppermute | solution.py:505
  83.6 0.0 collective-permute-done.12.above
  83.7 0.0 collective-permute-start.14
  83.7 3.5 %collective-permute-start.10 = (bf16[704,128]{1,0:T(8,128)(2,1)S(1)}, bf16[704,128]{1,0:T(8,128)(2,1)S(1)}, u32[]{:S(2)}, u32[]{:S(2)}) collective-permute-start(bf16[704,128]{1,0:T(8,128)(2,1)S(1)} %get-tuple-element.30), channel_id=1, source_target_pairs={{0,224},{32,64},{64,32},{96,128},{128,96},{160,192},{192,160},{224... | collective-permute-start | bytes 540680 | tf_op jit(solution)/shard_map/ppermute | solution.py:497
  87.2 0.0 collective-permute-start.9
  87.2 8.9 %collective-permute-done.9.other_front = bf16[640,128]{1,0:T(8,128)(2,1)S(1)} collective-permute-done((bf16[640,128]{1,0:T(8,128)(2,1)S(1)}, bf16[640,128]{1,0:T(8,128)(2,1)S(1)}, u32[]{:S(2)}, u32[]{:S(2)}) %collective-permute-start.9) | collective-permute-done | bytes 163872 | tf_op jit(solution)/shard_map/ppermute | solution.py:496
  96.1 0.0 collective-permute-start.15
  96.1 0.0 collective-permute-done.10.other_back
  96.1 4.8 %collective-permute-start.17 = (bf16[640,128]{1,0:T(8,128)(2,1)S(1)}, bf16[640,128]{1,0:T(8,128)(2,1)S(1)}, u32[]{:S(2)}, u32[]{:S(2)}) collective-permute-start(bf16[640,128]{1,0:T(8,128)(2,1)S(1)} %collective-permute-done.9.other_front), channel_id=1, source_target_pairs={{2,0},{4,2},{6,4},{8,6},{10,8},{12,10},{14,12},{16,14},{18,16},{20... | collective-permute-start | bytes 491528 | tf_op jit(solution)/shard_map/ppermute | solution.py:502
  100.9 0.0 collective-permute-done.8.sibling
  100.9 0.0 collective-permute-start.16
  100.9 0.0 collective-permute-done.13.below_sibling
  100.9 4.8 %collective-permute-start.18 = (bf16[704,128]{1,0:T(8,128)(2,1)S(1)}, bf16[704,128]{1,0:T(8,128)(2,1)S(1)}, u32[]{:S(2)}, u32[]{:S(2)}) collective-permute-start(bf16[704,128]{1,0:T(8,128)(2,1)S(1)} %collective-permute-done.10.other_back), channel_id=1, source_target_pairs={{2,0},{4,2},{6,4},{8,6},{10,8},{12,10},{14,12},{16,14},{18,16},{20... | collective-permute-start | bytes 540680 | tf_op jit(solution)/shard_map/ppermute | solution.py:504
  105.7 1.1 shard_map.50
  106.8 2.9 %shard_map.51.acc_in = f32[512,768]{1,0:T(8,128)S(1)} custom-call(s32[1]{0:T(128)} %bitcast.2.refs_0_.parity, f32[512,768]{1,0:T(8,128)S(1)} %get-tuple-element.27.acc_in, bf16[512,768]{1,0:T(8,128)(2,1)S(1)} %get-tuple-element.28.dev, bf16[1344,128]{1,0:T(8,128)(2,1)S(1)} %collective-permute-done.8.sibling, ...), custom_call_target="tpu_custom_call", output_to_operand_aliasing={{}: (1, {})} | custom-call | flops 1200000000 | bytes 1000000 | tf_op jit(solution)/shard_map/pallas_call | solution.py:429
  109.7 0.0 collective-permute-done.14.above_sibling
  109.7 1.1 shard_map.52.acc
  110.8 0.0 collective-permute-done.15.below_front
  110.8 0.0 collective-permute-done.17.above_front
  110.8 0.0 collective-permute-done.16.below_back
  110.8 0.0 collective-permute-done.18.above_back
  110.8 1.2 shard_map.53
  112.0 27.3 %all_to_all.11.back = bf16[8,64,768]{2,1,0:T(8,128)(2,1)S(1)} all-to-all(bf16[8,64,768]{2,1,0:T(8,128)(2,1)S(1)} %shard_map.53), channel_id=1, replica_groups=mesh['member'=8,'space'=16,'group'=2] {'member'}, dimensions={0} | all-to-all | bytes 1572864 | tf_op jit(solution)/shard_map/all_to_all | solution.py:515
  139.3 1.6 %restore.1 = bf16[1,64,3,4,512]{4,3,2,1,0:T(4,128)(2,1)} custom-call(bf16[8,64,768]{2,1,0:T(8,128)(2,1)S(1)} %all_to_all.11.back), custom_call_target="tpu_custom_call" | custom-call | flops 10000000 | bytes 1000000 | tf_op jit(solution)/shard_map/restore/pallas_call | solution.py:467
  (5 shorter events, 0.2 us)
Async XLA Ops:
  1.5 10.0 %collective-permute-start.4 = (bf16[8,32,512]{2,1,0:T(8,128)(2,1)S(1)}, bf16[8,32,512]{2,1,0:T(8,128)(2,1)S(1)}, u32[]{:S(2)}, u32[]{:S(2)}) collective-permute-start(bf16[8,32,512]{2,1,0:T(8,128)(2,1)S(1)} %pad_maximum_fusion.2), channel_id=1, source_target_pairs={{0,2},{2,4},{4,6},{6,8},{8,10},{10,12},{12,14},{14,16},{16,18},{18... | collective-permute-start | bytes 786440 | tf_op jit(solution)/shard_map/ppermute | solution.py:132
  3.7 7.8 %collective-permute-start.5 = (bf16[8,32,512]{2,1,0:T(8,128)(2,1)S(1)}, bf16[8,32,512]{2,1,0:T(8,128)(2,1)S(1)}, u32[]{:S(2)}, u32[]{:S(2)}) collective-permute-start(bf16[8,32,512]{2,1,0:T(8,128)(2,1)S(1)} %pad_maximum_fusion.3), channel_id=1, source_target_pairs={{2,0},{4,2},{6,4},{8,6},{10,8},{12,10},{14,12},{16,14},{18,16},{20... | collective-permute-start | bytes 786440 | tf_op jit(solution)/shard_map/ppermute | solution.py:132
  7.5 10.2 %collective-permute-start.1 = (bf16[8,32,512]{2,1,0:T(8,128)(2,1)S(1)}, bf16[8,32,512]{2,1,0:T(8,128)(2,1)S(1)}, u32[]{:S(2)}, u32[]{:S(2)}) collective-permute-start(bf16[8,32,512]{2,1,0:T(8,128)(2,1)S(1)} %pad_maximum_fusion.1), channel_id=1, source_target_pairs={{2,0},{4,2},{6,4},{8,6},{10,8},{12,10},{14,12},{16,14},{18,16},{20... | collective-permute-start | bytes 786440 | tf_op jit(solution)/shard_map/ppermute | solution.py:132
  9.0 9.7 %collective-permute-start = (bf16[8,32,512]{2,1,0:T(8,128)(2,1)S(1)}, bf16[8,32,512]{2,1,0:T(8,128)(2,1)S(1)}, u32[]{:S(2)}, u32[]{:S(2)}) collective-permute-start(bf16[8,32,512]{2,1,0:T(8,128)(2,1)S(1)} %pad_maximum_fusion), channel_id=1, source_target_pairs={{0,2},{2,4},{4,6},{6,8},{8,10},{10,12},{12,14},{14,16},{16,18},{18... | collective-permute-start | bytes 786440 | tf_op jit(solution)/shard_map/ppermute | solution.py:132
  12.8 12.2 %collective-permute-start.6 = (bf16[8,32,512]{2,1,0:T(8,128)(2,1)S(1)}, bf16[8,32,512]{2,1,0:T(8,128)(2,1)S(1)}, u32[]{:S(2)}, u32[]{:S(2)}) collective-permute-start(bf16[8,32,512]{2,1,0:T(8,128)(2,1)S(1)} %get-tuple-element.24), channel_id=1, source_target_pairs={{0,2},{2,4},{4,6},{6,8},{8,10},{10,12},{12,14},{14,16},{16,18},{18... | collective-permute-start | bytes 786440 | tf_op jit(solution)/shard_map/ppermute | solution.py:132
  13.4 11.6 %collective-permute-start.7 = (bf16[8,32,512]{2,1,0:T(8,128)(2,1)S(1)}, bf16[8,32,512]{2,1,0:T(8,128)(2,1)S(1)}, u32[]{:S(2)}, u32[]{:S(2)}) collective-permute-start(bf16[8,32,512]{2,1,0:T(8,128)(2,1)S(1)} %get-tuple-element.25), channel_id=1, source_target_pairs={{2,0},{4,2},{6,4},{8,6},{10,8},{12,10},{14,12},{16,14},{18,16},{20... | collective-permute-start | bytes 786440 | tf_op jit(solution)/shard_map/ppermute | solution.py:132
  20.1 10.3 %collective-permute-start.2 = (bf16[8,32,512]{2,1,0:T(8,128)(2,1)S(1)}, bf16[8,32,512]{2,1,0:T(8,128)(2,1)S(1)}, u32[]{:S(2)}, u32[]{:S(2)}) collective-permute-start(bf16[8,32,512]{2,1,0:T(8,128)(2,1)S(1)} %get-tuple-element.21), channel_id=1, source_target_pairs={{0,2},{2,4},{4,6},{6,8},{8,10},{10,12},{12,14},{14,16},{16,18},{18... | collective-permute-start | bytes 786440 | tf_op jit(solution)/shard_map/ppermute | solution.py:132
  20.1 10.3 %collective-permute-start.3 = (bf16[8,32,512]{2,1,0:T(8,128)(2,1)S(1)}, bf16[8,32,512]{2,1,0:T(8,128)(2,1)S(1)}, u32[]{:S(2)}, u32[]{:S(2)}) collective-permute-start(bf16[8,32,512]{2,1,0:T(8,128)(2,1)S(1)} %get-tuple-element.22), channel_id=1, source_target_pairs={{2,0},{4,2},{6,4},{8,6},{10,8},{12,10},{14,12},{16,14},{18,16},{20... | collective-permute-start | bytes 786440 | tf_op jit(solution)/shard_map/ppermute | solution.py:132
  30.4 32.9 %copy-start = (s32[1,1,8,256]{3,2,1,0:T(8,128)S(1)}, s32[1,1,8,256]{3,2,1,0:T(8,128)}, u32[]{:S(2)}) copy-start(s32[1,1,8,256]{3,2,1,0:T(8,128)} %param.5) | copy-start | bytes 24580
  30.4 32.9 %copy-start.1 = (f32[1,1,1,256]{3,2,1,0:T(1,128)S(1)}, f32[1,1,1,256]{3,2,1,0:T(1,128)}, u32[]{:S(2)}) copy-start(f32[1,1,1,256]{3,2,1,0:T(1,128)} %param.6) | copy-start | bytes 3076
  30.4 32.9 %copy-start.2 = (f32[1,1,1,256]{3,2,1,0:T(1,128)S(1)}, f32[1,1,1,256]{3,2,1,0:T(1,128)}, u32[]{:S(2)}) copy-start(f32[1,1,1,256]{3,2,1,0:T(1,128)} %param.7) | copy-start | bytes 3076
  69.3 9.8 %collective-permute-start.11 = (bf16[1344,128]{1,0:T(8,128)(2,1)S(1)}, bf16[1344,128]{1,0:T(8,128)(2,1)S(1)}, u32[]{:S(2)}, u32[]{:S(2)}) collective-permute-start(bf16[1344,128]{1,0:T(8,128)(2,1)S(1)} %get-tuple-element.26.refs_2_), channel_id=1, source_target_pairs={{0,2},{2,4},{4,6},{6,8},{8,10},{10,12},{12,14},{14,16},{16,18},{18... | collective-permute-start | bytes 1032200 | tf_op jit(solution)/shard_map/ppermute | solution.py:498
  69.4 14.2 %collective-permute-start.12 = (bf16[1344,128]{1,0:T(8,128)(2,1)S(1)}, bf16[1344,128]{1,0:T(8,128)(2,1)S(1)}, u32[]{:S(2)}, u32[]{:S(2)}) collective-permute-start(bf16[1344,128]{1,0:T(8,128)(2,1)S(1)} %get-tuple-element.26.refs_2_), channel_id=1, source_target_pairs={{2,0},{4,2},{6,4},{8,6},{10,8},{12,10},{14,12},{16,14},{18,16},{20... | collective-permute-start | bytes 1032200 | tf_op jit(solution)/shard_map/ppermute | solution.py:499
  74.6 26.3 %collective-permute-start.8 = (bf16[1344,128]{1,0:T(8,128)(2,1)S(1)}, bf16[1344,128]{1,0:T(8,128)(2,1)S(1)}, u32[]{:S(2)}, u32[]{:S(2)}) collective-permute-start(bf16[1344,128]{1,0:T(8,128)(2,1)S(1)} %get-tuple-element.26.refs_2_), channel_id=1, source_target_pairs={{0,32},{32,0},{64,96},{96,64},{128,160},{160,128},{192,224},{224,1... | collective-permute-start | bytes 1032200 | tf_op jit(solution)/shard_map/ppermute | solution.py:500
  79.1 21.8 %collective-permute-start.13 = (bf16[1344,128]{1,0:T(8,128)(2,1)S(1)}, bf16[1344,128]{1,0:T(8,128)(2,1)S(1)}, u32[]{:S(2)}, u32[]{:S(2)}) collective-permute-start(bf16[1344,128]{1,0:T(8,128)(2,1)S(1)} %collective-permute-done.11.below), channel_id=1, source_target_pairs={{0,32},{32,0},{64,96},{96,64},{128,160},{160,128},{192,224},{224,1... | collective-permute-start | bytes 1032200 | tf_op jit(solution)/shard_map/ppermute | solution.py:505
  83.7 26.1 %collective-permute-start.14 = (bf16[1344,128]{1,0:T(8,128)(2,1)S(1)}, bf16[1344,128]{1,0:T(8,128)(2,1)S(1)}, u32[]{:S(2)}, u32[]{:S(2)}) collective-permute-start(bf16[1344,128]{1,0:T(8,128)(2,1)S(1)} %collective-permute-done.12.above), channel_id=1, source_target_pairs={{0,32},{32,0},{64,96},{96,64},{128,160},{160,128},{192,224},{224,1... | collective-permute-start | bytes 1032200 | tf_op jit(solution)/shard_map/ppermute | solution.py:506
  83.7 12.4 %collective-permute-start.10 = (bf16[704,128]{1,0:T(8,128)(2,1)S(1)}, bf16[704,128]{1,0:T(8,128)(2,1)S(1)}, u32[]{:S(2)}, u32[]{:S(2)}) collective-permute-start(bf16[704,128]{1,0:T(8,128)(2,1)S(1)} %get-tuple-element.30), channel_id=1, source_target_pairs={{0,224},{32,64},{64,32},{96,128},{128,96},{160,192},{192,160},{224... | collective-permute-start | bytes 540680 | tf_op jit(solution)/shard_map/ppermute | solution.py:497
  87.2 8.9 %collective-permute-start.9 = (bf16[640,128]{1,0:T(8,128)(2,1)S(1)}, bf16[640,128]{1,0:T(8,128)(2,1)S(1)}, u32[]{:S(2)}, u32[]{:S(2)}) collective-permute-start(bf16[640,128]{1,0:T(8,128)(2,1)S(1)} %get-tuple-element.29), channel_id=1, source_target_pairs={{0,224},{32,64},{64,32},{96,128},{128,96},{160,192},{192,160},{224... | collective-permute-start | bytes 491528 | tf_op jit(solution)/shard_map/ppermute | solution.py:496
  96.1 14.7 %collective-permute-start.15 = (bf16[640,128]{1,0:T(8,128)(2,1)S(1)}, bf16[640,128]{1,0:T(8,128)(2,1)S(1)}, u32[]{:S(2)}, u32[]{:S(2)}) collective-permute-start(bf16[640,128]{1,0:T(8,128)(2,1)S(1)} %collective-permute-done.9.other_front), channel_id=1, source_target_pairs={{0,2},{2,4},{4,6},{6,8},{8,10},{10,12},{12,14},{14,16},{16,18},{18... | collective-permute-start | bytes 491528 | tf_op jit(solution)/shard_map/ppermute | solution.py:501
  96.1 14.7 %collective-permute-start.17 = (bf16[640,128]{1,0:T(8,128)(2,1)S(1)}, bf16[640,128]{1,0:T(8,128)(2,1)S(1)}, u32[]{:S(2)}, u32[]{:S(2)}) collective-permute-start(bf16[640,128]{1,0:T(8,128)(2,1)S(1)} %collective-permute-done.9.other_front), channel_id=1, source_target_pairs={{2,0},{4,2},{6,4},{8,6},{10,8},{12,10},{14,12},{16,14},{18,16},{20... | collective-permute-start | bytes 491528 | tf_op jit(solution)/shard_map/ppermute | solution.py:502
  100.9 9.9 %collective-permute-start.16 = (bf16[704,128]{1,0:T(8,128)(2,1)S(1)}, bf16[704,128]{1,0:T(8,128)(2,1)S(1)}, u32[]{:S(2)}, u32[]{:S(2)}) collective-permute-start(bf16[704,128]{1,0:T(8,128)(2,1)S(1)} %collective-permute-done.10.other_back), channel_id=1, source_target_pairs={{0,2},{2,4},{4,6},{6,8},{8,10},{10,12},{12,14},{14,16},{16,18},{18... | collective-permute-start | bytes 540680 | tf_op jit(solution)/shard_map/ppermute | solution.py:503
  100.9 9.9 %collective-permute-start.18 = (bf16[704,128]{1,0:T(8,128)(2,1)S(1)}, bf16[704,128]{1,0:T(8,128)(2,1)S(1)}, u32[]{:S(2)}, u32[]{:S(2)}) collective-permute-start(bf16[704,128]{1,0:T(8,128)(2,1)S(1)} %collective-permute-done.10.other_back), channel_id=1, source_target_pairs={{2,0},{4,2},{6,4},{8,6},{10,8},{12,10},{14,12},{16,14},{18,16},{20... | collective-permute-start | bytes 540680 | tf_op jit(solution)/shard_map/ppermute | solution.py:504

commit v2 on v1

--- a/solution.py
+++ b/solution.py
@@ -15,8 +15,7 @@
 BLOCK = 128
 PAIRS = [(i, j) for i in range(4) for j in range(i, 4)]
 CENTRE_AT = len(PAIRS) * BLOCK
-FRONT = len(PAIRS) // 2 * BLOCK
-PACKED = CENTRE_AT + 4 * 16
+PACKED = CENTRE_AT + 16
 
 time_step = 0.4
 coriolis = 0.3
@@ -200,16 +199,8 @@
 
 def weights_kernel(*refs):
     regions = refs[:HALVES]
-    tile, index, value, var, packed, front, back = refs[HALVES : HALVES + 7]
-    z_ref, zt_ref, b_ref, m_ref, l_ref, u_ref = refs[HALVES + 7 :]
-
-    def put(start, rows):
-        packed[start : start + rows.shape[0], :] = rows
-        if start < FRONT:
-            front[start : start + rows.shape[0], :] = rows
-        else:
-            back[start - FRONT : start - FRONT + rows.shape[0], :] = rows
-
+    tile, index, value, var, packed = refs[HALVES : HALVES + 5]
+    z_ref, zt_ref, b_ref, m_ref, l_ref, u_ref = refs[HALVES + 5 :]
     identity = eye(OBS)
 
     def as_column(row):
@@ -289,6 +280,7 @@
     m_parts = split(m * (scale * inverse_norm))
     small = eye(BLOCK)
     spot = lax.broadcasted_iota(jnp.int32, (16, BLOCK), 0)
+    both = jnp.zeros((16, BLOCK), f32)
     at = 0
     for i in range(4):
         v = product(split(z_ref[i * BLOCK : (i + 1) * BLOCK, :]), m_parts)
@@ -297,22 +289,20 @@
             block = band[:, (j - i) * BLOCK : (j - i + 1) * BLOCK]
             if i == j:
                 block = block + (scale * low) * small
-            put(at, block.astype(bf16))
+            packed[at : at + BLOCK, :] = block.astype(bf16)
             at += BLOCK
-        piece = centre[:, i * BLOCK : (i + 1) * BLOCK]
-        high = piece.astype(bf16).astype(f32)
-        both = jnp.where(spot == 0, high, jnp.where(spot == 1, piece - high, 0.0))
-        put(CENTRE_AT + 16 * i, both.astype(bf16))
+        along = centre[:, i * BLOCK : (i + 1) * BLOCK]
+        high = along.astype(bf16).astype(f32)
+        both = both + jnp.where(spot == i, high, jnp.where(spot == 4 + i, along - high, 0.0))
+    packed[CENTRE_AT:, :] = both.astype(bf16)
 
 
 def region_weights(regions, tile, index, values, variances):
     return pl.pallas_call(
         weights_kernel,
-        out_shape=[
-            jax.ShapeDtypeStruct((size, BLOCK), bf16) for size in (PACKED, FRONT, PACKED - FRONT)
-        ],
+        out_shape=jax.ShapeDtypeStruct((PACKED, BLOCK), bf16),
         in_specs=[vmem] * HALVES + [smem] + [vmem] * 3,
-        out_specs=[vmem] * 3,
+        out_specs=vmem,
         scratch_shapes=[
             pltpu.VMEM((MEMBERS, OBS), f32),
             pltpu.VMEM((OBS, MEMBERS), f32),
@@ -350,17 +340,9 @@
     return {(row, s): (r if row else 1.0 - r) * side[s] for row in (0, 1) for s in (0, 1, 2)}
 
 
-def piece(source, start, size):
-    if not isinstance(source, tuple):
-        return source[start : start + size, :]
-    if start < FRONT:
-        return source[0][start : start + size, :]
-    return source[1][start - FRONT : start - FRONT + size, :]
-
-
 def unpack(source, full):
     for n, (i, j) in enumerate(PAIRS):
-        block = piece(source, n * BLOCK, BLOCK)
+        block = source[n * BLOCK : (n + 1) * BLOCK, :]
         full[i * BLOCK : (i + 1) * BLOCK, j * BLOCK : (j + 1) * BLOCK] = block
         if i != j:
             turned = jnp.transpose(block)
@@ -369,8 +351,11 @@
 
 def apply(source, full, dev, acc, lo, hi, factor, before=None, out=None):
     unpack(source, full)
+    spot = lax.broadcasted_iota(jnp.int32, (16, BLOCK), 0)
+    centre = source[CENTRE_AT:, :].astype(f32)
     for i in range(4):
-        full[MEMBERS:, i * BLOCK : (i + 1) * BLOCK] = piece(source, CENTRE_AT + 16 * i, 16)
+        mine = jnp.where(spot % 4 == i, centre, 0.0)
+        full[MEMBERS:, i * BLOCK : (i + 1) * BLOCK] = mine.astype(bf16)
 
     def part(at):
         both = dot(full[...], dev[:, at])
@@ -402,11 +387,11 @@
 
 
 def near_kernel(
-    parity, acc_in, dev, sibling, other_front, other_back, below, above, acc, full
+    parity, acc_in, dev, sibling, other, below, above, acc, full
 ):
     factor = factors(parity[0])
     apply(sibling, full, dev, acc, 0, COLS, factor[0, 1])
-    apply((other_front, other_back), full, dev, acc, 0, COLS, factor[0, 2])
+    apply(other, full, dev, acc, 0, COLS, factor[0, 2])
     apply(below, full, dev, acc, 0, HALF, factor[1, 0])
     apply(above, full, dev, acc, HALF, COLS, factor[1, 0])
 
@@ -418,11 +403,11 @@
 
 
 def far_kernel(
-    parity, acc, dev, below_front, below_back, above_front, above_back, out, full
+    parity, acc, dev, below_other, above_other, out, full
 ):
     factor = factors(parity[0])
-    apply((below_front, below_back), full, dev, acc, 0, HALF, factor[1, 2], out=out)
-    apply((above_front, above_back), full, dev, acc, HALF, COLS, factor[1, 2], out=out)
+    apply(below_other, full, dev, acc, 0, HALF, factor[1, 2], out=out)
+    apply(above_other, full, dev, acc, HALF, COLS, factor[1, 2], out=out)
 
 
 def call(kernel, outs, flops, scratch, parity, *arrays, alias=False):
@@ -491,17 +476,14 @@
     chunks = forecast(fields, up, down)
     region = lax.all_to_all(chunks, "member", 0, 0, tiled=True).reshape(MEMBERS, COLS)
     regions = [region]
-    own, front, behind = region_weights(regions, tile.reshape(1), obs_index[0, 0], obs_value[0, 0], obs_var[0, 0])
-
-    other_front = lax.ppermute(front, "member", other_pairs)
-    other_back = lax.ppermute(behind, "member", other_pairs)
+    own = region_weights(regions, tile.reshape(1), obs_index[0, 0], obs_value[0, 0], obs_var[0, 0])
+
+    other = lax.ppermute(own, "member", other_pairs)
     below = lax.ppermute(own, "space", up)
     above = lax.ppermute(own, "space", down)
     sibling = lax.ppermute(own, "member", sibling_pairs)
-    below_front = lax.ppermute(other_front, "space", up)
-    above_front = lax.ppermute(other_front, "space", down)
-    below_back = lax.ppermute(other_back, "space", up)
-    above_back = lax.ppermute(other_back, "space", down)
+    below_other = lax.ppermute(other, "space", up)
+    above_other = lax.ppermute(other, "space", down)
     below_sibling = lax.ppermute(below, "member", sibling_pairs)
     above_sibling = lax.ppermute(above, "member", sibling_pairs)
     total_shape = jax.ShapeDtypeStruct((MEMBERS, COLS), f32)
@@ -509,9 +491,9 @@
     out_shape = jax.ShapeDtypeStruct((tiles, near_members, COLS), bf16)
     mean_scratch = [pltpu.VMEM((1, COLS), f32)]
     acc, dev = call(own_kernel, (total_shape, dev_shape), 400_000_000, mean_scratch, parity, *regions, own)
-    acc = call(near_kernel, total_shape, 1_200_000_000, [], parity, acc, dev, sibling, other_front, other_back, below, above, alias=True)
+    acc = call(near_kernel, total_shape, 1_200_000_000, [], parity, acc, dev, sibling, other, below, above, alias=True)
     acc = call(side_kernel, total_shape, 400_000_000, [], parity, acc, dev, below_sibling, above_sibling, alias=True)
-    analysed = call(far_kernel, out_shape, 400_000_000, [], parity, acc, dev, below_front, below_back, above_front, above_back)
+    analysed = call(far_kernel, out_shape, 400_000_000, [], parity, acc, dev, below_other, above_other)
     back = lax.all_to_all(analysed, "member", 0, 0, tiled=True)
     return restored(back)
 

time: 141 us -> 129 us (0.915)
  starting transfers between devices: 44.1 us -> 36.1 us
  waiting for transfers between devices: 16.9 us -> 11.8 us
  Pallas kernels: 19.4 us -> 21.1 us
    ppermute x6 -> x3, waiting for transfers between devices: 8.91 us -> 4.06 us  [the longest x1 4.06 us: program(): other = lax.ppermute(own, 'member', other_pairs)]
    ppermute x1, starting transfers between devices: 3.94 us -> 0.01 us  [program(): sibling = lax.ppermute(own, 'member', sibling_pairs)]
    ppermute x6 -> x3, starting transfers between devices: 13.1 us -> 9.2 us  [the longest x1 4.78 us: program(): above_other = lax.ppermute(other, 'space', down)]
  transfers between devices with their start and end apart: 19 -> 16, of which waited for: 5 -> 5; matrix products, arithmetic and copies ran while one was open for 0% -> 0% of each run, Pallas kernels for 7% -> 8%
where the time goes in v2:
time: 129 us
  blocking collectives  58.5 us (45%)
  starting transfers between devices  36.1 us (28%)
  Pallas kernels  21.1 us (16%)
  waiting for transfers between devices  11.8 us (9%)
  local copies, waits for them, and re-layouts  1.45 us (1%)
    all_to_all x1, blocking collectives, program(): lax.all_to_all(chunks, 'member', 0, 0, tiled=True).reshape(MEMBERS, COLS)  31.4 us
    all_to_all x1, blocking collectives, program(): back = lax.all_to_all(analysed, 'member', 0, 0, tiled=True)  27.1 us
    ppermute x8, starting transfers between devices, swapped(): return (lax.ppermute(last, 'space', up), lax.ppermute(first, 'space', down))  17.3 us
    ppermute x8, waiting for transfers between devices, swapped(): return (lax.ppermute(last, 'space', up), lax.ppermute(first, 'space', down))  7.41 us
    pallas_call x4, Pallas kernels, call(): pl.pallas_call(kernel, out_shape=outs, in_specs=[smem] + [vmem] * len(arr...  7.2 us
    pallas_call x1, Pallas kernels, region_weights(): pl.pallas_call(weights_kernel, out_shape=jax.ShapeDtypeStruct((PACKED, BL...  6.79 us
    pallas_call x4, Pallas kernels, step(): pl.pallas_call(kernel, out_shape=outs, in_specs=[vmem] * len(arrays), out...  5.54 us
    ppermute x1, starting transfers between devices, program(): above = lax.ppermute(own, 'space', down)  5.06 us
  transfers between devices with their start and end apart: 16, of which 5 were waited for; matrix products, arithmetic and copies ran while one was open for 0% of the time, Pallas kernels for 8%

profile of v2, /device:TPU:1, one launch (start us, length us, event | category | flops | bytes accessed | tf_op | source)
XLA Modules:
  0.0 129.2 jit_solution(10003430644825931166)
XLA Ops:
  0.0 1.3 copy.10
  1.3 0.1 slice_bitcast_fusion.1
  1.5 2.2 %collective-permute-start.4 = (bf16[8,32,512]{2,1,0:T(8,128)(2,1)S(1)}, bf16[8,32,512]{2,1,0:T(8,128)(2,1)S(1)}, u32[]{:S(2)}, u32[]{:S(2)}) collective-permute-start(bf16[8,32,512]{2,1,0:T(8,128)(2,1)S(1)} %pad_maximum_fusion.2), channel_id=1, source_target_pairs={{0,2},{2,4},{4,6},{6,8},{8,10},{10,12},{12,14},{14,16},{16,18},{18... | collective-permute-start | bytes 786440 | tf_op jit(solution)/shard_map/ppermute | solution.py:131
  3.7 3.7 %collective-permute-start.5 = (bf16[8,32,512]{2,1,0:T(8,128)(2,1)S(1)}, bf16[8,32,512]{2,1,0:T(8,128)(2,1)S(1)}, u32[]{:S(2)}, u32[]{:S(2)}) collective-permute-start(bf16[8,32,512]{2,1,0:T(8,128)(2,1)S(1)} %pad_maximum_fusion.3), channel_id=1, source_target_pairs={{2,0},{4,2},{6,4},{8,6},{10,8},{12,10},{14,12},{16,14},{18,16},{20... | collective-permute-start | bytes 786440 | tf_op jit(solution)/shard_map/ppermute | solution.py:131
  7.5 1.5 %collective-permute-start.1 = (bf16[8,32,512]{2,1,0:T(8,128)(2,1)S(1)}, bf16[8,32,512]{2,1,0:T(8,128)(2,1)S(1)}, u32[]{:S(2)}, u32[]{:S(2)}) collective-permute-start(bf16[8,32,512]{2,1,0:T(8,128)(2,1)S(1)} %pad_maximum_fusion.1), channel_id=1, source_target_pairs={{2,0},{4,2},{6,4},{8,6},{10,8},{12,10},{14,12},{16,14},{18,16},{20... | collective-permute-start | bytes 786440 | tf_op jit(solution)/shard_map/ppermute | solution.py:131
  9.0 0.1 collective-permute-start
  9.1 0.1 fusion
  9.2 2.3 %collective-permute-done.4.below = bf16[8,32,512]{2,1,0:T(8,128)(2,1)S(1)} collective-permute-done((bf16[8,32,512]{2,1,0:T(8,128)(2,1)S(1)}, bf16[8,32,512]{2,1,0:T(8,128)(2,1)S(1)}, u32[]{:S(2)}, u32[]{:S(2)}) %collective-permute-start.4) | collective-permute-done | bytes 262176 | tf_op jit(solution)/shard_map/ppermute | solution.py:131
  11.5 0.0 collective-permute-done.5.above
  11.5 1.3 %shard_map.47 = (f32[3,4,32,512]{3,2,1,0:T(8,128)S(1)}, bf16[8,32,512]{2,1,0:T(8,128)(2,1)S(1)}, bf16[8,32,512]{2,1,0:T(8,128)(2,1)S(1)}) custom-call(bf16[3,4,32,512]{3,2,1,0:T(8,128)(2,1)S(1)} %get-tuple-element.37.now, bf16[8,32,512]{2,1,0:T(8,128)(2,1)S(1)} %collective-permute-done.4.below, bf16[8,32,512]{2,1,0:T(8,128)(2,1)S(1)} %collective-permute-done.5.above), custom_call_target="tpu_custom_call" | custom-call | flops 50000000 | bytes 1000000 | tf_op jit(solution)/shard_map/pallas_call | solution.py:141
  12.8 0.6 collective-permute-start.6
  13.4 4.3 %collective-permute-start.7 = (bf16[8,32,512]{2,1,0:T(8,128)(2,1)S(1)}, bf16[8,32,512]{2,1,0:T(8,128)(2,1)S(1)}, u32[]{:S(2)}, u32[]{:S(2)}) collective-permute-start(bf16[8,32,512]{2,1,0:T(8,128)(2,1)S(1)} %get-tuple-element.22), channel_id=1, source_target_pairs={{2,0},{4,2},{6,4},{8,6},{10,8},{12,10},{14,12},{16,14},{18,16},{20... | collective-permute-start | bytes 786440 | tf_op jit(solution)/shard_map/ppermute | solution.py:131
  17.6 0.0 collective-permute-done.1.above
  17.6 1.1 collective-permute-done.below
  18.8 1.3 %shard_map.46 = (f32[3,4,32,512]{3,2,1,0:T(8,128)S(1)}, bf16[8,32,512]{2,1,0:T(8,128)(2,1)S(1)}, bf16[8,32,512]{2,1,0:T(8,128)(2,1)S(1)}) custom-call(bf16[3,4,32,512]{3,2,1,0:T(8,128)(2,1)S(1)} %get-tuple-element.38.now, bf16[8,32,512]{2,1,0:T(8,128)(2,1)S(1)} %collective-permute-done.below, bf16[8,32,512]{2,1,0:T(8,128)(2,1)S(1)} %collective-permute-done.1.above), custom_call_target="tpu_custom_call" | custom-call | flops 50000000 | bytes 1000000 | tf_op jit(solution)/shard_map/pallas_call | solution.py:141
  20.1 0.1 collective-permute-start.2
  20.1 4.8 %collective-permute-start.3 = (bf16[8,32,512]{2,1,0:T(8,128)(2,1)S(1)}, bf16[8,32,512]{2,1,0:T(8,128)(2,1)S(1)}, u32[]{:S(2)}, u32[]{:S(2)}) collective-permute-start(bf16[8,32,512]{2,1,0:T(8,128)(2,1)S(1)} %get-tuple-element.19), channel_id=1, source_target_pairs={{2,0},{4,2},{6,4},{8,6},{10,8},{12,10},{14,12},{16,14},{18,16},{20... | collective-permute-start | bytes 786440 | tf_op jit(solution)/shard_map/ppermute | solution.py:131
  24.9 0.0 collective-permute-done.6.below
  24.9 0.0 collective-permute-done.7.above
  24.9 1.5 %shard_map.48.refs_0_ = bf16[8,64,768]{2,1,0:T(8,128)(2,1)S(1)} custom-call(f32[3,4,32,512]{3,2,1,0:T(8,128)S(1)} %get-tuple-element.20.now, bf16[8,32,512]{2,1,0:T(8,128)(2,1)S(1)} %collective-permute-done.6.below, bf16[8,32,512]{2,1,0:T(8,128)(2,1)S(1)} %collective-permute-done.7.above), custom_call_target="tpu_custom_call" | custom-call | flops 50000000 | bytes 1000000 | tf_op jit(solution)/shard_map/pallas_call | solution.py:141
  26.4 4.0 %collective-permute-done.2.below = bf16[8,32,512]{2,1,0:T(8,128)(2,1)S(1)} collective-permute-done((bf16[8,32,512]{2,1,0:T(8,128)(2,1)S(1)}, bf16[8,32,512]{2,1,0:T(8,128)(2,1)S(1)}, u32[]{:S(2)}, u32[]{:S(2)}) %collective-permute-start.2) | collective-permute-done | bytes 262176 | tf_op jit(solution)/shard_map/ppermute | solution.py:131
  30.4 0.0 collective-permute-done.3.above
  30.4 0.0 copy-start
  30.4 0.0 copy-start.1
  30.4 0.0 copy-start.2
  30.4 1.5 %shard_map.49 = bf16[8,64,768]{2,1,0:T(8,128)(2,1)S(1)} custom-call(f32[3,4,32,512]{3,2,1,0:T(8,128)S(1)} %get-tuple-element.17.now, bf16[8,32,512]{2,1,0:T(8,128)(2,1)S(1)} %collective-permute-done.2.below, bf16[8,32,512]{2,1,0:T(8,128)(2,1)S(1)} %collective-permute-done.3.above, ...), custom_call_target="tpu_custom_call", output_to_operand_aliasing={{}: (3, {})} | custom-call | flops 50000000 | bytes 1000000 | tf_op jit(solution)/shard_map/pallas_call | solution.py:141
  31.9 31.4 %all_to_all.10 = bf16[8,64,768]{2,1,0:T(8,128)(2,1)S(1)} all-to-all(bf16[8,64,768]{2,1,0:T(8,128)(2,1)S(1)} %shard_map.49), channel_id=1, replica_groups=mesh['member'=8,'space'=16,'group'=2] {'member'}, dimensions={0} | all-to-all | bytes 1572864 | tf_op jit(solution)/shard_map/all_to_all | solution.py:477
  63.3 0.0 copy-done
  63.3 0.0 copy-done.1
  63.3 0.0 copy-done.2
  63.3 6.8 %weights.1.refs_2_ = bf16[1296,128]{1,0:T(8,128)(2,1)} custom-call(bf16[512,768]{1,0:T(8,128)(2,1)S(1)} %bitcast.35, s32[1]{0:T(128)} %bitcast.16.refs_1_, s32[8,256]{1,0:T(8,128)S(1)} %bitcast.37, f32[1,256]{1,0:T(1,128)S(1)} %bitcast.38, f32[1,256]{1,0:T(1,128)S(1)} %bitcast.39), custom_call_target="tpu_custom_call" | custom-call | flops 6000000000 | bytes 1000000 | tf_op jit(solution)/shard_map/weights/pallas_call | solution.py:301
  70.1 0.0 collective-permute-start.10
  70.1 5.1 %collective-permute-start.11 = (bf16[1296,128]{1,0:T(8,128)(2,1)}, bf16[1296,128]{1,0:T(8,128)(2,1)S(1)}, u32[]{:S(2)}, u32[]{:S(2)}) collective-permute-start(bf16[1296,128]{1,0:T(8,128)(2,1)} %weights.1.refs_2_), channel_id=1, source_target_pairs={{2,0},{4,2},{6,4},{8,6},{10,8},{12,10},{14,12},{16,14},{18,16},{20... | collective-permute-start | bytes 995336 | tf_op jit(solution)/shard_map/ppermute | solution.py:483
  75.1 4.4 %collective-permute-start.9 = (bf16[1296,128]{1,0:T(8,128)(2,1)}, bf16[1296,128]{1,0:T(8,128)(2,1)S(1)}, u32[]{:S(2)}, u32[]{:S(2)}) collective-permute-start(bf16[1296,128]{1,0:T(8,128)(2,1)} %weights.1.refs_2_), channel_id=1, source_target_pairs={{0,224},{32,64},{64,32},{96,128},{128,96},{160,192},{192,160},{224... | collective-permute-start | bytes 995336 | tf_op jit(solution)/shard_map/ppermute | solution.py:481
  79.5 0.0 collective-permute-start.8
  79.5 0.3 collective-permute-done.10.below
  79.8 4.5 %collective-permute-start.12 = (bf16[1296,128]{1,0:T(8,128)(2,1)S(1)}, bf16[1296,128]{1,0:T(8,128)(2,1)S(1)}, u32[]{:S(2)}, u32[]{:S(2)}) collective-permute-start(bf16[1296,128]{1,0:T(8,128)(2,1)S(1)} %collective-permute-done.10.below), channel_id=1, source_target_pairs={{0,32},{32,0},{64,96},{96,64},{128,160},{160,128},{192,224},{224,1... | collective-permute-start | bytes 995336 | tf_op jit(solution)/shard_map/ppermute | solution.py:487
  84.4 0.0 collective-permute-done.11.above
  84.4 0.0 collective-permute-start.13
  84.4 4.1 %collective-permute-done.9.other = bf16[1296,128]{1,0:T(8,128)(2,1)S(1)} collective-permute-done((bf16[1296,128]{1,0:T(8,128)(2,1)}, bf16[1296,128]{1,0:T(8,128)(2,1)S(1)}, u32[]{:S(2)}, u32[]{:S(2)}) %collective-permute-start.9) | collective-permute-done | bytes 331808 | tf_op jit(solution)/shard_map/ppermute | solution.py:481
  88.4 0.0 collective-permute-start.14
  88.4 4.8 %collective-permute-start.15 = (bf16[1296,128]{1,0:T(8,128)(2,1)S(1)}, bf16[1296,128]{1,0:T(8,128)(2,1)S(1)}, u32[]{:S(2)}, u32[]{:S(2)}) collective-permute-start(bf16[1296,128]{1,0:T(8,128)(2,1)S(1)} %collective-permute-done.9.other), channel_id=1, source_target_pairs={{2,0},{4,2},{6,4},{8,6},{10,8},{12,10},{14,12},{16,14},{18,16},{20... | collective-permute-start | bytes 995336 | tf_op jit(solution)/shard_map/ppermute | solution.py:486
  93.2 2.1 %shard_map.50 = (f32[512,768]{1,0:T(8,128)S(1)}, bf16[512,768]{1,0:T(8,128)(2,1)S(1)}) custom-call(s32[1]{0:T(128)} %bitcast.2.refs_0_.parity, bf16[512,768]{1,0:T(8,128)(2,1)S(1)} %bitcast.36, bf16[1296,128]{1,0:T(8,128)(2,1)} %weights.1.refs_2_), custom_call_target="tpu_custom_call" | custom-call | flops 400000000 | bytes 1000000 | tf_op jit(solution)/shard_map/pallas_call | solution.py:414
  95.3 0.0 collective-permute-done.8.sibling
  95.4 2.9 %shard_map.51.acc_in = f32[512,768]{1,0:T(8,128)S(1)} custom-call(s32[1]{0:T(128)} %bitcast.2.refs_0_.parity, f32[512,768]{1,0:T(8,128)S(1)} %get-tuple-element.23.acc_in, bf16[512,768]{1,0:T(8,128)(2,1)S(1)} %get-tuple-element.24.dev, bf16[1296,128]{1,0:T(8,128)(2,1)S(1)} %collective-permute-done.8.sibling, ...), custom_call_target="tpu_custom_call", output_to_operand_aliasing={{}: (1, {})} | custom-call | flops 1200000000 | bytes 1000000 | tf_op jit(solution)/shard_map/pallas_call | solution.py:414
  98.2 0.0 collective-permute-done.12.below_sibling
  98.2 0.0 collective-permute-done.13.above_sibling
  98.2 1.1 shard_map.52.acc
  99.3 0.0 collective-permute-done.14.below_other
  99.3 0.0 collective-permute-done.15.above_other
  99.3 1.1 shard_map.53
  100.5 27.1 %all_to_all.11.back = bf16[8,64,768]{2,1,0:T(8,128)(2,1)S(1)} all-to-all(bf16[8,64,768]{2,1,0:T(8,128)(2,1)S(1)} %shard_map.53), channel_id=1, replica_groups=mesh['member'=8,'space'=16,'group'=2] {'member'}, dimensions={0} | all-to-all | bytes 1572864 | tf_op jit(solution)/shard_map/all_to_all | solution.py:497
  127.6 1.6 %restore.1 = bf16[1,64,3,4,512]{4,3,2,1,0:T(4,128)(2,1)} custom-call(bf16[8,64,768]{2,1,0:T(8,128)(2,1)S(1)} %all_to_all.11.back), custom_call_target="tpu_custom_call" | custom-call | flops 10000000 | bytes 1000000 | tf_op jit(solution)/shard_map/restore/pallas_call | solution.py:452
  (5 shorter events, 0.2 us)
Async XLA Ops:
  1.5 10.0 %collective-permute-start.4 = (bf16[8,32,512]{2,1,0:T(8,128)(2,1)S(1)}, bf16[8,32,512]{2,1,0:T(8,128)(2,1)S(1)}, u32[]{:S(2)}, u32[]{:S(2)}) collective-permute-start(bf16[8,32,512]{2,1,0:T(8,128)(2,1)S(1)} %pad_maximum_fusion.2), channel_id=1, source_target_pairs={{0,2},{2,4},{4,6},{6,8},{8,10},{10,12},{12,14},{14,16},{16,18},{18... | collective-permute-start | bytes 786440 | tf_op jit(solution)/shard_map/ppermute | solution.py:131
  3.7 7.8 %collective-permute-start.5 = (bf16[8,32,512]{2,1,0:T(8,128)(2,1)S(1)}, bf16[8,32,512]{2,1,0:T(8,128)(2,1)S(1)}, u32[]{:S(2)}, u32[]{:S(2)}) collective-permute-start(bf16[8,32,512]{2,1,0:T(8,128)(2,1)S(1)} %pad_maximum_fusion.3), channel_id=1, source_target_pairs={{2,0},{4,2},{6,4},{8,6},{10,8},{12,10},{14,12},{16,14},{18,16},{20... | collective-permute-start | bytes 786440 | tf_op jit(solution)/shard_map/ppermute | solution.py:131
  7.5 10.2 %collective-permute-start.1 = (bf16[8,32,512]{2,1,0:T(8,128)(2,1)S(1)}, bf16[8,32,512]{2,1,0:T(8,128)(2,1)S(1)}, u32[]{:S(2)}, u32[]{:S(2)}) collective-permute-start(bf16[8,32,512]{2,1,0:T(8,128)(2,1)S(1)} %pad_maximum_fusion.1), channel_id=1, source_target_pairs={{2,0},{4,2},{6,4},{8,6},{10,8},{12,10},{14,12},{16,14},{18,16},{20... | collective-permute-start | bytes 786440 | tf_op jit(solution)/shard_map/ppermute | solution.py:131
  9.0 9.7 %collective-permute-start = (bf16[8,32,512]{2,1,0:T(8,128)(2,1)S(1)}, bf16[8,32,512]{2,1,0:T(8,128)(2,1)S(1)}, u32[]{:S(2)}, u32[]{:S(2)}) collective-permute-start(bf16[8,32,512]{2,1,0:T(8,128)(2,1)S(1)} %pad_maximum_fusion), channel_id=1, source_target_pairs={{0,2},{2,4},{4,6},{6,8},{8,10},{10,12},{12,14},{14,16},{16,18},{18... | collective-permute-start | bytes 786440 | tf_op jit(solution)/shard_map/ppermute | solution.py:131
  12.8 12.2 %collective-permute-start.6 = (bf16[8,32,512]{2,1,0:T(8,128)(2,1)S(1)}, bf16[8,32,512]{2,1,0:T(8,128)(2,1)S(1)}, u32[]{:S(2)}, u32[]{:S(2)}) collective-permute-start(bf16[8,32,512]{2,1,0:T(8,128)(2,1)S(1)} %get-tuple-element.21), channel_id=1, source_target_pairs={{0,2},{2,4},{4,6},{6,8},{8,10},{10,12},{12,14},{14,16},{16,18},{18... | collective-permute-start | bytes 786440 | tf_op jit(solution)/shard_map/ppermute | solution.py:131
  13.4 11.6 %collective-permute-start.7 = (bf16[8,32,512]{2,1,0:T(8,128)(2,1)S(1)}, bf16[8,32,512]{2,1,0:T(8,128)(2,1)S(1)}, u32[]{:S(2)}, u32[]{:S(2)}) collective-permute-start(bf16[8,32,512]{2,1,0:T(8,128)(2,1)S(1)} %get-tuple-element.22), channel_id=1, source_target_pairs={{2,0},{4,2},{6,4},{8,6},{10,8},{12,10},{14,12},{16,14},{18,16},{20... | collective-permute-start | bytes 786440 | tf_op jit(solution)/shard_map/ppermute | solution.py:131
  20.1 10.3 %collective-permute-start.2 = (bf16[8,32,512]{2,1,0:T(8,128)(2,1)S(1)}, bf16[8,32,512]{2,1,0:T(8,128)(2,1)S(1)}, u32[]{:S(2)}, u32[]{:S(2)}) collective-permute-start(bf16[8,32,512]{2,1,0:T(8,128)(2,1)S(1)} %get-tuple-element.18), channel_id=1, source_target_pairs={{0,2},{2,4},{4,6},{6,8},{8,10},{10,12},{12,14},{14,16},{16,18},{18... | collective-permute-start | bytes 786440 | tf_op jit(solution)/shard_map/ppermute | solution.py:131
  20.1 10.3 %collective-permute-start.3 = (bf16[8,32,512]{2,1,0:T(8,128)(2,1)S(1)}, bf16[8,32,512]{2,1,0:T(8,128)(2,1)S(1)}, u32[]{:S(2)}, u32[]{:S(2)}) collective-permute-start(bf16[8,32,512]{2,1,0:T(8,128)(2,1)S(1)} %get-tuple-element.19), channel_id=1, source_target_pairs={{2,0},{4,2},{6,4},{8,6},{10,8},{12,10},{14,12},{16,14},{18,16},{20... | collective-permute-start | bytes 786440 | tf_op jit(solution)/shard_map/ppermute | solution.py:131
  30.4 32.9 %copy-start = (s32[1,1,8,256]{3,2,1,0:T(8,128)S(1)}, s32[1,1,8,256]{3,2,1,0:T(8,128)}, u32[]{:S(2)}) copy-start(s32[1,1,8,256]{3,2,1,0:T(8,128)} %param.5) | copy-start | bytes 24580
  30.4 32.9 %copy-start.1 = (f32[1,1,1,256]{3,2,1,0:T(1,128)S(1)}, f32[1,1,1,256]{3,2,1,0:T(1,128)}, u32[]{:S(2)}) copy-start(f32[1,1,1,256]{3,2,1,0:T(1,128)} %param.6) | copy-start | bytes 3076
  30.4 32.9 %copy-start.2 = (f32[1,1,1,256]{3,2,1,0:T(1,128)S(1)}, f32[1,1,1,256]{3,2,1,0:T(1,128)}, u32[]{:S(2)}) copy-start(f32[1,1,1,256]{3,2,1,0:T(1,128)} %param.7) | copy-start | bytes 3076
  70.1 9.8 %collective-permute-start.10 = (bf16[1296,128]{1,0:T(8,128)(2,1)}, bf16[1296,128]{1,0:T(8,128)(2,1)S(1)}, u32[]{:S(2)}, u32[]{:S(2)}) collective-permute-start(bf16[1296,128]{1,0:T(8,128)(2,1)} %weights.1.refs_2_), channel_id=1, source_target_pairs={{0,2},{2,4},{4,6},{6,8},{8,10},{10,12},{12,14},{14,16},{16,18},{18... | collective-permute-start | bytes 995336 | tf_op jit(solution)/shard_map/ppermute | solution.py:482
  70.1 14.3 %collective-permute-start.11 = (bf16[1296,128]{1,0:T(8,128)(2,1)}, bf16[1296,128]{1,0:T(8,128)(2,1)S(1)}, u32[]{:S(2)}, u32[]{:S(2)}) collective-permute-start(bf16[1296,128]{1,0:T(8,128)(2,1)} %weights.1.refs_2_), channel_id=1, source_target_pairs={{2,0},{4,2},{6,4},{8,6},{10,8},{12,10},{14,12},{16,14},{18,16},{20... | collective-permute-start | bytes 995336 | tf_op jit(solution)/shard_map/ppermute | solution.py:483
  75.1 13.3 %collective-permute-start.9 = (bf16[1296,128]{1,0:T(8,128)(2,1)}, bf16[1296,128]{1,0:T(8,128)(2,1)S(1)}, u32[]{:S(2)}, u32[]{:S(2)}) collective-permute-start(bf16[1296,128]{1,0:T(8,128)(2,1)} %weights.1.refs_2_), channel_id=1, source_target_pairs={{0,224},{32,64},{64,32},{96,128},{128,96},{160,192},{192,160},{224... | collective-permute-start | bytes 995336 | tf_op jit(solution)/shard_map/ppermute | solution.py:481
  79.5 15.8 %collective-permute-start.8 = (bf16[1296,128]{1,0:T(8,128)(2,1)}, bf16[1296,128]{1,0:T(8,128)(2,1)S(1)}, u32[]{:S(2)}, u32[]{:S(2)}) collective-permute-start(bf16[1296,128]{1,0:T(8,128)(2,1)} %weights.1.refs_2_), channel_id=1, source_target_pairs={{0,32},{32,0},{64,96},{96,64},{128,160},{160,128},{192,224},{224,1... | collective-permute-start | bytes 995336 | tf_op jit(solution)/shard_map/ppermute | solution.py:484
  79.8 18.4 %collective-permute-start.12 = (bf16[1296,128]{1,0:T(8,128)(2,1)S(1)}, bf16[1296,128]{1,0:T(8,128)(2,1)S(1)}, u32[]{:S(2)}, u32[]{:S(2)}) collective-permute-start(bf16[1296,128]{1,0:T(8,128)(2,1)S(1)} %collective-permute-done.10.below), channel_id=1, source_target_pairs={{0,32},{32,0},{64,96},{96,64},{128,160},{160,128},{192,224},{224,1... | collective-permute-start | bytes 995336 | tf_op jit(solution)/shard_map/ppermute | solution.py:487
  84.4 13.9 %collective-permute-start.13 = (bf16[1296,128]{1,0:T(8,128)(2,1)S(1)}, bf16[1296,128]{1,0:T(8,128)(2,1)S(1)}, u32[]{:S(2)}, u32[]{:S(2)}) collective-permute-start(bf16[1296,128]{1,0:T(8,128)(2,1)S(1)} %collective-permute-done.11.above), channel_id=1, source_target_pairs={{0,32},{32,0},{64,96},{96,64},{128,160},{160,128},{192,224},{224,1... | collective-permute-start | bytes 995336 | tf_op jit(solution)/shard_map/ppermute | solution.py:488
  88.4 10.9 %collective-permute-start.14 = (bf16[1296,128]{1,0:T(8,128)(2,1)S(1)}, bf16[1296,128]{1,0:T(8,128)(2,1)S(1)}, u32[]{:S(2)}, u32[]{:S(2)}) collective-permute-start(bf16[1296,128]{1,0:T(8,128)(2,1)S(1)} %collective-permute-done.9.other), channel_id=1, source_target_pairs={{0,2},{2,4},{4,6},{6,8},{8,10},{10,12},{12,14},{14,16},{16,18},{18... | collective-permute-start | bytes 995336 | tf_op jit(solution)/shard_map/ppermute | solution.py:485
  88.4 10.9 %collective-permute-start.15 = (bf16[1296,128]{1,0:T(8,128)(2,1)S(1)}, bf16[1296,128]{1,0:T(8,128)(2,1)S(1)}, u32[]{:S(2)}, u32[]{:S(2)}) collective-permute-start(bf16[1296,128]{1,0:T(8,128)(2,1)S(1)} %collective-permute-done.9.other), channel_id=1, source_target_pairs={{2,0},{4,2},{6,4},{8,6},{10,8},{12,10},{14,12},{16,14},{18,16},{20... | collective-permute-start | bytes 995336 | tf_op jit(solution)/shard_map/ppermute | solution.py:486

commit v3 on v2

--- a/solution.py
+++ b/solution.py
@@ -14,7 +14,8 @@
 OBS = 256
 BLOCK = 128
 PAIRS = [(i, j) for i in range(4) for j in range(i, 4)]
-CENTRE_AT = len(PAIRS) * BLOCK
+SPOTS = {pair: n * BLOCK for n, pair in enumerate(PAIRS)}
+CENTRE_AT = SPOTS[3, 3]
 PACKED = CENTRE_AT + 16
 
 time_step = 0.4
@@ -289,8 +290,15 @@
             block = band[:, (j - i) * BLOCK : (j - i + 1) * BLOCK]
             if i == j:
                 block = block + (scale * low) * small
-            packed[at : at + BLOCK, :] = block.astype(bf16)
-            at += BLOCK
+            if i < 3:
+                packed[at : at + BLOCK, :] = block.astype(bf16)
+                at += BLOCK
+                continue
+            turned = pltpu.roll(block, 64, 1)
+            quarters = (block[:64, :64], turned[:64, :64], turned[64:, :64])
+            for d, quarter in enumerate(quarters):
+                start = SPOTS[d, d] + 64
+                packed[start : start + 64, :64] = quarter.astype(bf16)
         along = centre[:, i * BLOCK : (i + 1) * BLOCK]
         high = along.astype(bf16).astype(f32)
         both = both + jnp.where(spot == i, high, jnp.where(spot == 4 + i, along - high, 0.0))
@@ -341,12 +349,26 @@
 
 
 def unpack(source, full):
-    for n, (i, j) in enumerate(PAIRS):
-        block = source[n * BLOCK : (n + 1) * BLOCK, :]
+    row = lax.broadcasted_iota(jnp.int32, (BLOCK, BLOCK), 0)
+    col = lax.broadcasted_iota(jnp.int32, (BLOCK, BLOCK), 1)
+    free = (row >= 64) & (col < 64)
+
+    def mirrored(block):
+        return jnp.where(free, jnp.transpose(block), block).astype(bf16)
+
+    for i, j in PAIRS[:-1]:
+        block = source[SPOTS[i, j] : SPOTS[i, j] + BLOCK, :]
+        if i == j:
+            block = mirrored(block.astype(f32))
+        else:
+            full[j * BLOCK : (j + 1) * BLOCK, i * BLOCK : (i + 1) * BLOCK] = jnp.transpose(block)
         full[i * BLOCK : (i + 1) * BLOCK, j * BLOCK : (j + 1) * BLOCK] = block
-        if i != j:
-            turned = jnp.transpose(block)
-            full[j * BLOCK : (j + 1) * BLOCK, i * BLOCK : (i + 1) * BLOCK] = turned
+    x, y, z = (
+        source[SPOTS[d, d] + 64 : SPOTS[d, d] + BLOCK, :].astype(f32) for d in range(3)
+    )
+    top = jnp.where(col[:64] < 64, x, pltpu.roll(y, 64, 1))
+    block = jnp.concatenate([top, pltpu.roll(z, 64, 1)], axis=0)
+    full[3 * BLOCK : MEMBERS, 3 * BLOCK :] = mirrored(block)
 
 
 def apply(source, full, dev, acc, lo, hi, factor, before=None, out=None):

time: 129 us -> 128 us (level)
  Pallas kernels: 21.1 us -> 19.7 us
  transfers between devices with their start and end apart: 16 -> 16, of which waited for: 5 -> 4; matrix products, arithmetic and copies ran while one was open for 0% -> 0% of each run, Pallas kernels for 8% -> 7%
where the time goes in v3:
time: 128 us; the launch traced here: 127 us
  blocking collectives  58.9 us (46%)
  starting transfers between devices  35.9 us (28%)
  Pallas kernels  19.7 us (15%)
  waiting for transfers between devices  11.2 us (9%)
  local copies, waits for them, and re-layouts  1.45 us (1%)
    all_to_all x1, blocking collectives, program(): lax.all_to_all(chunks, 'member', 0, 0, tiled=True).reshape(MEMBERS, COLS)  31.4 us
    all_to_all x1, blocking collectives, program(): back = lax.all_to_all(analysed, 'member', 0, 0, tiled=True)  27.5 us
    ppermute x8, starting transfers between devices, swapped(): return (lax.ppermute(last, 'space', up), lax.ppermute(first, 'space', down))  17.3 us
    ppermute x8, waiting for transfers between devices, swapped(): return (lax.ppermute(last, 'space', up), lax.ppermute(first, 'space', down))  7.41 us
    pallas_call x4, Pallas kernels, call(): pl.pallas_call(kernel, out_shape=outs, in_specs=[smem] + [vmem] * len(arr...  6.43 us
    pallas_call x1, Pallas kernels, region_weights(): pl.pallas_call(weights_kernel, out_shape=jax.ShapeDtypeStruct((PACKED, BL...  6.14 us
    pallas_call x4, Pallas kernels, step(): pl.pallas_call(kernel, out_shape=outs, in_specs=[vmem] * len(arrays), out...  5.54 us
    ppermute x1, starting transfers between devices, program(): above = lax.ppermute(own, 'space', down)  5.13 us
  transfers between devices with their start and end apart: 16, of which 4 were waited for; matrix products, arithmetic and copies ran while one was open for 0% of the time, Pallas kernels for 7%

profile of v3, /device:TPU:1, one launch (start us, length us, event | category | flops | bytes accessed | tf_op | source)
XLA Modules:
  0.0 127.4 jit_solution(18085605184493644456)
XLA Ops:
  0.0 1.3 %copy.10 = bf16[1,64,3,4,512]{4,1,3,2,0:T(8,128)(2,1)S(1)} copy(bf16[1,64,3,4,512]{4,3,2,1,0:T(4,128)(2,1)} %param.4) | data formatting | bytes 1572864 | tf_op args[0]
  1.3 0.1 slice_bitcast_fusion.1
  1.5 2.2 %collective-permute-start.4 = (bf16[8,32,512]{2,1,0:T(8,128)(2,1)S(1)}, bf16[8,32,512]{2,1,0:T(8,128)(2,1)S(1)}, u32[]{:S(2)}, u32[]{:S(2)}) collective-permute-start(bf16[8,32,512]{2,1,0:T(8,128)(2,1)S(1)} %pad_maximum_fusion.2), channel_id=1, source_target_pairs={{0,2},{2,4},{4,6},{6,8},{8,10},{10,12},{12,14},{14,16},{16,18},{18... | collective-permute-start | bytes 786440 | tf_op jit(solution)/shard_map/ppermute | solution.py:132
  3.7 3.7 %collective-permute-start.5 = (bf16[8,32,512]{2,1,0:T(8,128)(2,1)S(1)}, bf16[8,32,512]{2,1,0:T(8,128)(2,1)S(1)}, u32[]{:S(2)}, u32[]{:S(2)}) collective-permute-start(bf16[8,32,512]{2,1,0:T(8,128)(2,1)S(1)} %pad_maximum_fusion.3), channel_id=1, source_target_pairs={{2,0},{4,2},{6,4},{8,6},{10,8},{12,10},{14,12},{16,14},{18,16},{20... | collective-permute-start | bytes 786440 | tf_op jit(solution)/shard_map/ppermute | solution.py:132
  7.5 1.5 %collective-permute-start.1 = (bf16[8,32,512]{2,1,0:T(8,128)(2,1)S(1)}, bf16[8,32,512]{2,1,0:T(8,128)(2,1)S(1)}, u32[]{:S(2)}, u32[]{:S(2)}) collective-permute-start(bf16[8,32,512]{2,1,0:T(8,128)(2,1)S(1)} %pad_maximum_fusion.1), channel_id=1, source_target_pairs={{2,0},{4,2},{6,4},{8,6},{10,8},{12,10},{14,12},{16,14},{18,16},{20... | collective-permute-start | bytes 786440 | tf_op jit(solution)/shard_map/ppermute | solution.py:132
  9.0 0.1 collective-permute-start
  9.1 0.1 fusion
  9.2 2.3 %collective-permute-done.4.below = bf16[8,32,512]{2,1,0:T(8,128)(2,1)S(1)} collective-permute-done((bf16[8,32,512]{2,1,0:T(8,128)(2,1)S(1)}, bf16[8,32,512]{2,1,0:T(8,128)(2,1)S(1)}, u32[]{:S(2)}, u32[]{:S(2)}) %collective-permute-start.4) | collective-permute-done | bytes 262176 | tf_op jit(solution)/shard_map/ppermute | solution.py:132
  11.5 0.0 collective-permute-done.5.above
  11.5 1.3 %shard_map.47 = (f32[3,4,32,512]{3,2,1,0:T(8,128)S(1)}, bf16[8,32,512]{2,1,0:T(8,128)(2,1)S(1)}, bf16[8,32,512]{2,1,0:T(8,128)(2,1)S(1)}) custom-call(bf16[3,4,32,512]{3,2,1,0:T(8,128)(2,1)S(1)} %get-tuple-element.37.now, bf16[8,32,512]{2,1,0:T(8,128)(2,1)S(1)} %collective-permute-done.4.below, bf16[8,32,512]{2,1,0:T(8,128)(2,1)S(1)} %collective-permute-done.5.above), custom_call_target="tpu_custom_call" | custom-call | flops 50000000 | bytes 1000000 | tf_op jit(solution)/shard_map/pallas_call | solution.py:142
  12.8 0.6 collective-permute-start.6
  13.4 4.3 %collective-permute-start.7 = (bf16[8,32,512]{2,1,0:T(8,128)(2,1)S(1)}, bf16[8,32,512]{2,1,0:T(8,128)(2,1)S(1)}, u32[]{:S(2)}, u32[]{:S(2)}) collective-permute-start(bf16[8,32,512]{2,1,0:T(8,128)(2,1)S(1)} %get-tuple-element.22), channel_id=1, source_target_pairs={{2,0},{4,2},{6,4},{8,6},{10,8},{12,10},{14,12},{16,14},{18,16},{20... | collective-permute-start | bytes 786440 | tf_op jit(solution)/shard_map/ppermute | solution.py:132
  17.6 0.0 collective-permute-done.1.above
  17.6 1.1 collective-permute-done.below
  18.8 1.3 %shard_map.46 = (f32[3,4,32,512]{3,2,1,0:T(8,128)S(1)}, bf16[8,32,512]{2,1,0:T(8,128)(2,1)S(1)}, bf16[8,32,512]{2,1,0:T(8,128)(2,1)S(1)}) custom-call(bf16[3,4,32,512]{3,2,1,0:T(8,128)(2,1)S(1)} %get-tuple-element.38.now, bf16[8,32,512]{2,1,0:T(8,128)(2,1)S(1)} %collective-permute-done.below, bf16[8,32,512]{2,1,0:T(8,128)(2,1)S(1)} %collective-permute-done.1.above), custom_call_target="tpu_custom_call" | custom-call | flops 50000000 | bytes 1000000 | tf_op jit(solution)/shard_map/pallas_call | solution.py:142
  20.1 0.1 collective-permute-start.2
  20.1 4.8 %collective-permute-start.3 = (bf16[8,32,512]{2,1,0:T(8,128)(2,1)S(1)}, bf16[8,32,512]{2,1,0:T(8,128)(2,1)S(1)}, u32[]{:S(2)}, u32[]{:S(2)}) collective-permute-start(bf16[8,32,512]{2,1,0:T(8,128)(2,1)S(1)} %get-tuple-element.19), channel_id=1, source_target_pairs={{2,0},{4,2},{6,4},{8,6},{10,8},{12,10},{14,12},{16,14},{18,16},{20... | collective-permute-start | bytes 786440 | tf_op jit(solution)/shard_map/ppermute | solution.py:132
  24.9 0.0 collective-permute-done.6.below
  24.9 0.0 collective-permute-done.7.above
  24.9 1.5 %shard_map.48.refs_0_ = bf16[8,64,768]{2,1,0:T(8,128)(2,1)S(1)} custom-call(f32[3,4,32,512]{3,2,1,0:T(8,128)S(1)} %get-tuple-element.20.now, bf16[8,32,512]{2,1,0:T(8,128)(2,1)S(1)} %collective-permute-done.6.below, bf16[8,32,512]{2,1,0:T(8,128)(2,1)S(1)} %collective-permute-done.7.above), custom_call_target="tpu_custom_call" | custom-call | flops 50000000 | bytes 1000000 | tf_op jit(solution)/shard_map/pallas_call | solution.py:142
  26.4 4.0 %collective-permute-done.2.below = bf16[8,32,512]{2,1,0:T(8,128)(2,1)S(1)} collective-permute-done((bf16[8,32,512]{2,1,0:T(8,128)(2,1)S(1)}, bf16[8,32,512]{2,1,0:T(8,128)(2,1)S(1)}, u32[]{:S(2)}, u32[]{:S(2)}) %collective-permute-start.2) | collective-permute-done | bytes 262176 | tf_op jit(solution)/shard_map/ppermute | solution.py:132
  30.4 0.0 collective-permute-done.3.above
  30.4 0.0 copy-start
  30.4 0.0 copy-start.1
  30.4 0.0 copy-start.2
  30.4 1.5 %shard_map.49 = bf16[8,64,768]{2,1,0:T(8,128)(2,1)S(1)} custom-call(f32[3,4,32,512]{3,2,1,0:T(8,128)S(1)} %get-tuple-element.17.now, bf16[8,32,512]{2,1,0:T(8,128)(2,1)S(1)} %collective-permute-done.2.below, bf16[8,32,512]{2,1,0:T(8,128)(2,1)S(1)} %collective-permute-done.3.above, ...), custom_call_target="tpu_custom_call", output_to_operand_aliasing={{}: (3, {})} | custom-call | flops 50000000 | bytes 1000000 | tf_op jit(solution)/shard_map/pallas_call | solution.py:142
  31.9 31.4 %all_to_all.10 = bf16[8,64,768]{2,1,0:T(8,128)(2,1)S(1)} all-to-all(bf16[8,64,768]{2,1,0:T(8,128)(2,1)S(1)} %shard_map.49), channel_id=1, replica_groups=mesh['member'=8,'space'=16,'group'=2] {'member'}, dimensions={0} | all-to-all | bytes 1572864 | tf_op jit(solution)/shard_map/all_to_all | solution.py:499
  63.3 0.0 copy-done
  63.3 0.0 copy-done.1
  63.3 0.0 copy-done.2
  63.3 6.1 %weights.1.refs_2_ = bf16[1168,128]{1,0:T(8,128)(2,1)S(1)} custom-call(bf16[512,768]{1,0:T(8,128)(2,1)S(1)} %bitcast.35, s32[1]{0:T(128)} %bitcast.16.refs_1_, s32[8,256]{1,0:T(8,128)S(1)} %bitcast.37, f32[1,256]{1,0:T(1,128)S(1)} %bitcast.38, f32[1,256]{1,0:T(1,128)S(1)} %bitcast.39), custom_call_target="tpu_custom_call" | custom-call | flops 6000000000 | bytes 1000000 | tf_op jit(solution)/shard_map/weights/pallas_call | solution.py:309
  69.4 0.1 collective-permute-start.10
  69.5 5.1 %collective-permute-start.11 = (bf16[1168,128]{1,0:T(8,128)(2,1)S(1)}, bf16[1168,128]{1,0:T(8,128)(2,1)S(1)}, u32[]{:S(2)}, u32[]{:S(2)}) collective-permute-start(bf16[1168,128]{1,0:T(8,128)(2,1)S(1)} %weights.1.refs_2_), channel_id=1, source_target_pairs={{2,0},{4,2},{6,4},{8,6},{10,8},{12,10},{14,12},{16,14},{18,16},{20... | collective-permute-start | bytes 897032 | tf_op jit(solution)/shard_map/ppermute | solution.py:505
  74.6 4.4 %collective-permute-start.9 = (bf16[1168,128]{1,0:T(8,128)(2,1)S(1)}, bf16[1168,128]{1,0:T(8,128)(2,1)S(1)}, u32[]{:S(2)}, u32[]{:S(2)}) collective-permute-start(bf16[1168,128]{1,0:T(8,128)(2,1)S(1)} %weights.1.refs_2_), channel_id=1, source_target_pairs={{0,224},{32,64},{64,32},{96,128},{128,96},{160,192},{192,160},{224... | collective-permute-start | bytes 897032 | tf_op jit(solution)/shard_map/ppermute | solution.py:503
  79.0 0.0 collective-permute-start.8
  79.0 0.0 collective-permute-done.10.below
  79.0 4.2 %collective-permute-start.12 = (bf16[1168,128]{1,0:T(8,128)(2,1)S(1)}, bf16[1168,128]{1,0:T(8,128)(2,1)S(1)}, u32[]{:S(2)}, u32[]{:S(2)}) collective-permute-start(bf16[1168,128]{1,0:T(8,128)(2,1)S(1)} %collective-permute-done.10.below), channel_id=1, source_target_pairs={{0,32},{32,0},{64,96},{96,64},{128,160},{160,128},{192,224},{224,1... | collective-permute-start | bytes 897032 | tf_op jit(solution)/shard_map/ppermute | solution.py:509
  83.2 0.0 collective-permute-done.11.above
  83.2 0.0 collective-permute-start.13
  83.2 3.8 %collective-permute-done.9.other = bf16[1168,128]{1,0:T(8,128)(2,1)S(1)} collective-permute-done((bf16[1168,128]{1,0:T(8,128)(2,1)S(1)}, bf16[1168,128]{1,0:T(8,128)(2,1)S(1)}, u32[]{:S(2)}, u32[]{:S(2)}) %collective-permute-start.9) | collective-permute-done | bytes 299040 | tf_op jit(solution)/shard_map/ppermute | solution.py:503
  87.0 0.0 collective-permute-start.14
  87.0 4.8 %collective-permute-start.15 = (bf16[1168,128]{1,0:T(8,128)(2,1)S(1)}, bf16[1168,128]{1,0:T(8,128)(2,1)S(1)}, u32[]{:S(2)}, u32[]{:S(2)}) collective-permute-start(bf16[1168,128]{1,0:T(8,128)(2,1)S(1)} %collective-permute-done.9.other), channel_id=1, source_target_pairs={{2,0},{4,2},{6,4},{8,6},{10,8},{12,10},{14,12},{16,14},{18,16},{20... | collective-permute-start | bytes 897032 | tf_op jit(solution)/shard_map/ppermute | solution.py:508
  91.8 1.2 shard_map.50
  93.0 0.0 collective-permute-done.8.sibling
  93.0 2.9 %shard_map.51.acc_in = f32[512,768]{1,0:T(8,128)S(1)} custom-call(s32[1]{0:T(128)} %bitcast.2.refs_0_.parity, f32[512,768]{1,0:T(8,128)S(1)} %get-tuple-element.23.acc_in, bf16[512,768]{1,0:T(8,128)(2,1)S(1)} %get-tuple-element.24.dev, bf16[1168,128]{1,0:T(8,128)(2,1)S(1)} %collective-permute-done.8.sibling, ...), custom_call_target="tpu_custom_call", output_to_operand_aliasing={{}: (1, {})} | custom-call | flops 1200000000 | bytes 1000000 | tf_op jit(solution)/shard_map/pallas_call | solution.py:436
  95.9 0.0 collective-permute-done.12.below_sibling
  95.9 0.0 collective-permute-done.13.above_sibling
  95.9 1.1 shard_map.52.acc
  97.1 0.0 collective-permute-done.14.below_other
  97.1 0.0 collective-permute-done.15.above_other
  97.1 1.2 shard_map.53
  98.3 27.5 %all_to_all.11.back = bf16[8,64,768]{2,1,0:T(8,128)(2,1)S(1)} all-to-all(bf16[8,64,768]{2,1,0:T(8,128)(2,1)S(1)} %shard_map.53), channel_id=1, replica_groups=mesh['member'=8,'space'=16,'group'=2] {'member'}, dimensions={0} | all-to-all | bytes 1572864 | tf_op jit(solution)/shard_map/all_to_all | solution.py:519
  125.8 1.6 %restore.1 = bf16[1,64,3,4,512]{4,3,2,1,0:T(4,128)(2,1)} custom-call(bf16[8,64,768]{2,1,0:T(8,128)(2,1)S(1)} %all_to_all.11.back), custom_call_target="tpu_custom_call" | custom-call | flops 10000000 | bytes 1000000 | tf_op jit(solution)/shard_map/restore/pallas_call | solution.py:474
  (5 shorter events, 0.2 us)
Async XLA Ops:
  1.5 10.0 %collective-permute-start.4 = (bf16[8,32,512]{2,1,0:T(8,128)(2,1)S(1)}, bf16[8,32,512]{2,1,0:T(8,128)(2,1)S(1)}, u32[]{:S(2)}, u32[]{:S(2)}) collective-permute-start(bf16[8,32,512]{2,1,0:T(8,128)(2,1)S(1)} %pad_maximum_fusion.2), channel_id=1, source_target_pairs={{0,2},{2,4},{4,6},{6,8},{8,10},{10,12},{12,14},{14,16},{16,18},{18... | collective-permute-start | bytes 786440 | tf_op jit(solution)/shard_map/ppermute | solution.py:132
  3.7 7.8 %collective-permute-start.5 = (bf16[8,32,512]{2,1,0:T(8,128)(2,1)S(1)}, bf16[8,32,512]{2,1,0:T(8,128)(2,1)S(1)}, u32[]{:S(2)}, u32[]{:S(2)}) collective-permute-start(bf16[8,32,512]{2,1,0:T(8,128)(2,1)S(1)} %pad_maximum_fusion.3), channel_id=1, source_target_pairs={{2,0},{4,2},{6,4},{8,6},{10,8},{12,10},{14,12},{16,14},{18,16},{20... | collective-permute-start | bytes 786440 | tf_op jit(solution)/shard_map/ppermute | solution.py:132
  7.5 10.2 %collective-permute-start.1 = (bf16[8,32,512]{2,1,0:T(8,128)(2,1)S(1)}, bf16[8,32,512]{2,1,0:T(8,128)(2,1)S(1)}, u32[]{:S(2)}, u32[]{:S(2)}) collective-permute-start(bf16[8,32,512]{2,1,0:T(8,128)(2,1)S(1)} %pad_maximum_fusion.1), channel_id=1, source_target_pairs={{2,0},{4,2},{6,4},{8,6},{10,8},{12,10},{14,12},{16,14},{18,16},{20... | collective-permute-start | bytes 786440 | tf_op jit(solution)/shard_map/ppermute | solution.py:132
  9.0 9.7 %collective-permute-start = (bf16[8,32,512]{2,1,0:T(8,128)(2,1)S(1)}, bf16[8,32,512]{2,1,0:T(8,128)(2,1)S(1)}, u32[]{:S(2)}, u32[]{:S(2)}) collective-permute-start(bf16[8,32,512]{2,1,0:T(8,128)(2,1)S(1)} %pad_maximum_fusion), channel_id=1, source_target_pairs={{0,2},{2,4},{4,6},{6,8},{8,10},{10,12},{12,14},{14,16},{16,18},{18... | collective-permute-start | bytes 786440 | tf_op jit(solution)/shard_map/ppermute | solution.py:132
  12.8 12.2 %collective-permute-start.6 = (bf16[8,32,512]{2,1,0:T(8,128)(2,1)S(1)}, bf16[8,32,512]{2,1,0:T(8,128)(2,1)S(1)}, u32[]{:S(2)}, u32[]{:S(2)}) collective-permute-start(bf16[8,32,512]{2,1,0:T(8,128)(2,1)S(1)} %get-tuple-element.21), channel_id=1, source_target_pairs={{0,2},{2,4},{4,6},{6,8},{8,10},{10,12},{12,14},{14,16},{16,18},{18... | collective-permute-start | bytes 786440 | tf_op jit(solution)/shard_map/ppermute | solution.py:132
  13.4 11.6 %collective-permute-start.7 = (bf16[8,32,512]{2,1,0:T(8,128)(2,1)S(1)}, bf16[8,32,512]{2,1,0:T(8,128)(2,1)S(1)}, u32[]{:S(2)}, u32[]{:S(2)}) collective-permute-start(bf16[8,32,512]{2,1,0:T(8,128)(2,1)S(1)} %get-tuple-element.22), channel_id=1, source_target_pairs={{2,0},{4,2},{6,4},{8,6},{10,8},{12,10},{14,12},{16,14},{18,16},{20... | collective-permute-start | bytes 786440 | tf_op jit(solution)/shard_map/ppermute | solution.py:132
  20.1 10.3 %collective-permute-start.2 = (bf16[8,32,512]{2,1,0:T(8,128)(2,1)S(1)}, bf16[8,32,512]{2,1,0:T(8,128)(2,1)S(1)}, u32[]{:S(2)}, u32[]{:S(2)}) collective-permute-start(bf16[8,32,512]{2,1,0:T(8,128)(2,1)S(1)} %get-tuple-element.18), channel_id=1, source_target_pairs={{0,2},{2,4},{4,6},{6,8},{8,10},{10,12},{12,14},{14,16},{16,18},{18... | collective-permute-start | bytes 786440 | tf_op jit(solution)/shard_map/ppermute | solution.py:132
  20.1 10.3 %collective-permute-start.3 = (bf16[8,32,512]{2,1,0:T(8,128)(2,1)S(1)}, bf16[8,32,512]{2,1,0:T(8,128)(2,1)S(1)}, u32[]{:S(2)}, u32[]{:S(2)}) collective-permute-start(bf16[8,32,512]{2,1,0:T(8,128)(2,1)S(1)} %get-tuple-element.19), channel_id=1, source_target_pairs={{2,0},{4,2},{6,4},{8,6},{10,8},{12,10},{14,12},{16,14},{18,16},{20... | collective-permute-start | bytes 786440 | tf_op jit(solution)/shard_map/ppermute | solution.py:132
  30.4 32.9 %copy-start = (s32[1,1,8,256]{3,2,1,0:T(8,128)S(1)}, s32[1,1,8,256]{3,2,1,0:T(8,128)}, u32[]{:S(2)}) copy-start(s32[1,1,8,256]{3,2,1,0:T(8,128)} %param.5) | copy-start | bytes 24580
  30.4 32.9 %copy-start.1 = (f32[1,1,1,256]{3,2,1,0:T(1,128)S(1)}, f32[1,1,1,256]{3,2,1,0:T(1,128)}, u32[]{:S(2)}) copy-start(f32[1,1,1,256]{3,2,1,0:T(1,128)} %param.6) | copy-start | bytes 3076
  30.4 32.9 %copy-start.2 = (f32[1,1,1,256]{3,2,1,0:T(1,128)S(1)}, f32[1,1,1,256]{3,2,1,0:T(1,128)}, u32[]{:S(2)}) copy-start(f32[1,1,1,256]{3,2,1,0:T(1,128)} %param.7) | copy-start | bytes 3076
  69.4 9.6 %collective-permute-start.10 = (bf16[1168,128]{1,0:T(8,128)(2,1)S(1)}, bf16[1168,128]{1,0:T(8,128)(2,1)S(1)}, u32[]{:S(2)}, u32[]{:S(2)}) collective-permute-start(bf16[1168,128]{1,0:T(8,128)(2,1)S(1)} %weights.1.refs_2_), channel_id=1, source_target_pairs={{0,2},{2,4},{4,6},{6,8},{8,10},{10,12},{12,14},{14,16},{16,18},{18... | collective-permute-start | bytes 897032 | tf_op jit(solution)/shard_map/ppermute | solution.py:504
  69.5 13.7 %collective-permute-start.11 = (bf16[1168,128]{1,0:T(8,128)(2,1)S(1)}, bf16[1168,128]{1,0:T(8,128)(2,1)S(1)}, u32[]{:S(2)}, u32[]{:S(2)}) collective-permute-start(bf16[1168,128]{1,0:T(8,128)(2,1)S(1)} %weights.1.refs_2_), channel_id=1, source_target_pairs={{2,0},{4,2},{6,4},{8,6},{10,8},{12,10},{14,12},{16,14},{18,16},{20... | collective-permute-start | bytes 897032 | tf_op jit(solution)/shard_map/ppermute | solution.py:505
  74.6 12.4 %collective-permute-start.9 = (bf16[1168,128]{1,0:T(8,128)(2,1)S(1)}, bf16[1168,128]{1,0:T(8,128)(2,1)S(1)}, u32[]{:S(2)}, u32[]{:S(2)}) collective-permute-start(bf16[1168,128]{1,0:T(8,128)(2,1)S(1)} %weights.1.refs_2_), channel_id=1, source_target_pairs={{0,224},{32,64},{64,32},{96,128},{128,96},{160,192},{192,160},{224... | collective-permute-start | bytes 897032 | tf_op jit(solution)/shard_map/ppermute | solution.py:503
  79.0 14.0 %collective-permute-start.8 = (bf16[1168,128]{1,0:T(8,128)(2,1)S(1)}, bf16[1168,128]{1,0:T(8,128)(2,1)S(1)}, u32[]{:S(2)}, u32[]{:S(2)}) collective-permute-start(bf16[1168,128]{1,0:T(8,128)(2,1)S(1)} %weights.1.refs_2_), channel_id=1, source_target_pairs={{0,32},{32,0},{64,96},{96,64},{128,160},{160,128},{192,224},{224,1... | collective-permute-start | bytes 897032 | tf_op jit(solution)/shard_map/ppermute | solution.py:506
  79.0 16.9 %collective-permute-start.12 = (bf16[1168,128]{1,0:T(8,128)(2,1)S(1)}, bf16[1168,128]{1,0:T(8,128)(2,1)S(1)}, u32[]{:S(2)}, u32[]{:S(2)}) collective-permute-start(bf16[1168,128]{1,0:T(8,128)(2,1)S(1)} %collective-permute-done.10.below), channel_id=1, source_target_pairs={{0,32},{32,0},{64,96},{96,64},{128,160},{160,128},{192,224},{224,1... | collective-permute-start | bytes 897032 | tf_op jit(solution)/shard_map/ppermute | solution.py:509
  83.2 12.7 %collective-permute-start.13 = (bf16[1168,128]{1,0:T(8,128)(2,1)S(1)}, bf16[1168,128]{1,0:T(8,128)(2,1)S(1)}, u32[]{:S(2)}, u32[]{:S(2)}) collective-permute-start(bf16[1168,128]{1,0:T(8,128)(2,1)S(1)} %collective-permute-done.11.above), channel_id=1, source_target_pairs={{0,32},{32,0},{64,96},{96,64},{128,160},{160,128},{192,224},{224,1... | collective-permute-start | bytes 897032 | tf_op jit(solution)/shard_map/ppermute | solution.py:510
  87.0 10.1 %collective-permute-start.14 = (bf16[1168,128]{1,0:T(8,128)(2,1)S(1)}, bf16[1168,128]{1,0:T(8,128)(2,1)S(1)}, u32[]{:S(2)}, u32[]{:S(2)}) collective-permute-start(bf16[1168,128]{1,0:T(8,128)(2,1)S(1)} %collective-permute-done.9.other), channel_id=1, source_target_pairs={{0,2},{2,4},{4,6},{6,8},{8,10},{10,12},{12,14},{14,16},{16,18},{18... | collective-permute-start | bytes 897032 | tf_op jit(solution)/shard_map/ppermute | solution.py:507
  87.0 10.1 %collective-permute-start.15 = (bf16[1168,128]{1,0:T(8,128)(2,1)S(1)}, bf16[1168,128]{1,0:T(8,128)(2,1)S(1)}, u32[]{:S(2)}, u32[]{:S(2)}) collective-permute-start(bf16[1168,128]{1,0:T(8,128)(2,1)S(1)} %collective-permute-done.9.other), channel_id=1, source_target_pairs={{2,0},{4,2},{6,4},{8,6},{10,8},{12,10},{14,12},{16,14},{18,16},{20... | collective-permute-start | bytes 897032 | tf_op jit(solution)/shard_map/ppermute | solution.py:508

commit v4 on v3

--- a/solution.py
+++ b/solution.py
@@ -283,9 +283,12 @@
     spot = lax.broadcasted_iota(jnp.int32, (16, BLOCK), 0)
     both = jnp.zeros((16, BLOCK), f32)
     at = 0
+    v_high, v_low = split(product(split(z_ref[...]), m_parts))
+    zt_high, zt_low = split(zt_ref[...])
     for i in range(4):
-        v = product(split(z_ref[i * BLOCK : (i + 1) * BLOCK, :]), m_parts)
-        band = product(split(v), split(zt_ref[:, i * BLOCK :]))
+        rows = slice(i * BLOCK, (i + 1) * BLOCK)
+        right = (zt_high[:, i * BLOCK :], zt_low[:, i * BLOCK :])
+        band = product((v_high[rows], v_low[rows]), right)
         for j in range(i, 4):
             block = band[:, (j - i) * BLOCK : (j - i + 1) * BLOCK]
             if i == j:

time: 128 us -> 128 us (level)
  no operation moved by 1% of the time
where the time goes in v4:
time: 128 us; the launch traced here: 127 us
  blocking collectives  58.9 us (46%)
  starting transfers between devices  35.9 us (28%)
  Pallas kernels  19.8 us (15%)
  waiting for transfers between devices  11.2 us (9%)
  local copies, waits for them, and re-layouts  1.45 us (1%)
    all_to_all x1, blocking collectives, program(): lax.all_to_all(chunks, 'member', 0, 0, tiled=True).reshape(MEMBERS, COLS)  31.4 us
    all_to_all x1, blocking collectives, program(): back = lax.all_to_all(analysed, 'member', 0, 0, tiled=True)  27.5 us
    ppermute x8, starting transfers between devices, swapped(): return (lax.ppermute(last, 'space', up), lax.ppermute(first, 'space', down))  17.3 us
    ppermute x8, waiting for transfers between devices, swapped(): return (lax.ppermute(last, 'space', up), lax.ppermute(first, 'space', down))  7.41 us
    pallas_call x4, Pallas kernels, call(): pl.pallas_call(kernel, out_shape=outs, in_specs=[smem] + [vmem] * len(arr...  6.43 us
    pallas_call x1, Pallas kernels, region_weights(): pl.pallas_call(weights_kernel, out_shape=jax.ShapeDtypeStruct((PACKED, BL...  6.23 us
    pallas_call x4, Pallas kernels, step(): pl.pallas_call(kernel, out_shape=outs, in_specs=[vmem] * len(arrays), out...  5.54 us
    ppermute x1, starting transfers between devices, program(): above = lax.ppermute(own, 'space', down)  5.13 us
  transfers between devices with their start and end apart: 16, of which 4 were waited for; matrix products, arithmetic and copies ran while one was open for 0% of the time, Pallas kernels for 7%

profile of v4, /device:TPU:1, one launch (start us, length us, event | category | flops | bytes accessed | tf_op | source)
XLA Modules:
  0.0 127.5 jit_solution(3734771905055903587)
XLA Ops:
  0.0 1.3 %copy.10 = bf16[1,64,3,4,512]{4,1,3,2,0:T(8,128)(2,1)S(1)} copy(bf16[1,64,3,4,512]{4,3,2,1,0:T(4,128)(2,1)} %param.4) | data formatting | bytes 1572864 | tf_op args[0]
  1.3 0.1 slice_bitcast_fusion.1
  1.5 2.2 %collective-permute-start.4 = (bf16[8,32,512]{2,1,0:T(8,128)(2,1)S(1)}, bf16[8,32,512]{2,1,0:T(8,128)(2,1)S(1)}, u32[]{:S(2)}, u32[]{:S(2)}) collective-permute-start(bf16[8,32,512]{2,1,0:T(8,128)(2,1)S(1)} %pad_maximum_fusion.2), channel_id=1, source_target_pairs={{0,2},{2,4},{4,6},{6,8},{8,10},{10,12},{12,14},{14,16},{16,18},{18... | collective-permute-start | bytes 786440 | tf_op jit(solution)/shard_map/ppermute | solution.py:132
  3.7 3.7 %collective-permute-start.5 = (bf16[8,32,512]{2,1,0:T(8,128)(2,1)S(1)}, bf16[8,32,512]{2,1,0:T(8,128)(2,1)S(1)}, u32[]{:S(2)}, u32[]{:S(2)}) collective-permute-start(bf16[8,32,512]{2,1,0:T(8,128)(2,1)S(1)} %pad_maximum_fusion.3), channel_id=1, source_target_pairs={{2,0},{4,2},{6,4},{8,6},{10,8},{12,10},{14,12},{16,14},{18,16},{20... | collective-permute-start | bytes 786440 | tf_op jit(solution)/shard_map/ppermute | solution.py:132
  7.5 1.5 %collective-permute-start.1 = (bf16[8,32,512]{2,1,0:T(8,128)(2,1)S(1)}, bf16[8,32,512]{2,1,0:T(8,128)(2,1)S(1)}, u32[]{:S(2)}, u32[]{:S(2)}) collective-permute-start(bf16[8,32,512]{2,1,0:T(8,128)(2,1)S(1)} %pad_maximum_fusion.1), channel_id=1, source_target_pairs={{2,0},{4,2},{6,4},{8,6},{10,8},{12,10},{14,12},{16,14},{18,16},{20... | collective-permute-start | bytes 786440 | tf_op jit(solution)/shard_map/ppermute | solution.py:132
  9.0 0.1 collective-permute-start
  9.1 0.1 fusion
  9.2 2.3 %collective-permute-done.4.below = bf16[8,32,512]{2,1,0:T(8,128)(2,1)S(1)} collective-permute-done((bf16[8,32,512]{2,1,0:T(8,128)(2,1)S(1)}, bf16[8,32,512]{2,1,0:T(8,128)(2,1)S(1)}, u32[]{:S(2)}, u32[]{:S(2)}) %collective-permute-start.4) | collective-permute-done | bytes 262176 | tf_op jit(solution)/shard_map/ppermute | solution.py:132
  11.5 0.0 collective-permute-done.5.above
  11.5 1.3 %shard_map.47 = (f32[3,4,32,512]{3,2,1,0:T(8,128)S(1)}, bf16[8,32,512]{2,1,0:T(8,128)(2,1)S(1)}, bf16[8,32,512]{2,1,0:T(8,128)(2,1)S(1)}) custom-call(bf16[3,4,32,512]{3,2,1,0:T(8,128)(2,1)S(1)} %get-tuple-element.37.now, bf16[8,32,512]{2,1,0:T(8,128)(2,1)S(1)} %collective-permute-done.4.below, bf16[8,32,512]{2,1,0:T(8,128)(2,1)S(1)} %collective-permute-done.5.above), custom_call_target="tpu_custom_call" | custom-call | flops 50000000 | bytes 1000000 | tf_op jit(solution)/shard_map/pallas_call | solution.py:142
  12.8 0.6 collective-permute-start.6
  13.4 4.3 %collective-permute-start.7 = (bf16[8,32,512]{2,1,0:T(8,128)(2,1)S(1)}, bf16[8,32,512]{2,1,0:T(8,128)(2,1)S(1)}, u32[]{:S(2)}, u32[]{:S(2)}) collective-permute-start(bf16[8,32,512]{2,1,0:T(8,128)(2,1)S(1)} %get-tuple-element.22), channel_id=1, source_target_pairs={{2,0},{4,2},{6,4},{8,6},{10,8},{12,10},{14,12},{16,14},{18,16},{20... | collective-permute-start | bytes 786440 | tf_op jit(solution)/shard_map/ppermute | solution.py:132
  17.6 0.0 collective-permute-done.1.above
  17.6 1.1 collective-permute-done.below
  18.8 1.3 %shard_map.46 = (f32[3,4,32,512]{3,2,1,0:T(8,128)S(1)}, bf16[8,32,512]{2,1,0:T(8,128)(2,1)S(1)}, bf16[8,32,512]{2,1,0:T(8,128)(2,1)S(1)}) custom-call(bf16[3,4,32,512]{3,2,1,0:T(8,128)(2,1)S(1)} %get-tuple-element.38.now, bf16[8,32,512]{2,1,0:T(8,128)(2,1)S(1)} %collective-permute-done.below, bf16[8,32,512]{2,1,0:T(8,128)(2,1)S(1)} %collective-permute-done.1.above), custom_call_target="tpu_custom_call" | custom-call | flops 50000000 | bytes 1000000 | tf_op jit(solution)/shard_map/pallas_call | solution.py:142
  20.1 0.1 collective-permute-start.2
  20.1 4.8 %collective-permute-start.3 = (bf16[8,32,512]{2,1,0:T(8,128)(2,1)S(1)}, bf16[8,32,512]{2,1,0:T(8,128)(2,1)S(1)}, u32[]{:S(2)}, u32[]{:S(2)}) collective-permute-start(bf16[8,32,512]{2,1,0:T(8,128)(2,1)S(1)} %get-tuple-element.19), channel_id=1, source_target_pairs={{2,0},{4,2},{6,4},{8,6},{10,8},{12,10},{14,12},{16,14},{18,16},{20... | collective-permute-start | bytes 786440 | tf_op jit(solution)/shard_map/ppermute | solution.py:132
  24.9 0.0 collective-permute-done.6.below
  24.9 0.0 collective-permute-done.7.above
  24.9 1.5 %shard_map.48.refs_0_ = bf16[8,64,768]{2,1,0:T(8,128)(2,1)S(1)} custom-call(f32[3,4,32,512]{3,2,1,0:T(8,128)S(1)} %get-tuple-element.20.now, bf16[8,32,512]{2,1,0:T(8,128)(2,1)S(1)} %collective-permute-done.6.below, bf16[8,32,512]{2,1,0:T(8,128)(2,1)S(1)} %collective-permute-done.7.above), custom_call_target="tpu_custom_call" | custom-call | flops 50000000 | bytes 1000000 | tf_op jit(solution)/shard_map/pallas_call | solution.py:142
  26.4 4.0 %collective-permute-done.2.below = bf16[8,32,512]{2,1,0:T(8,128)(2,1)S(1)} collective-permute-done((bf16[8,32,512]{2,1,0:T(8,128)(2,1)S(1)}, bf16[8,32,512]{2,1,0:T(8,128)(2,1)S(1)}, u32[]{:S(2)}, u32[]{:S(2)}) %collective-permute-start.2) | collective-permute-done | bytes 262176 | tf_op jit(solution)/shard_map/ppermute | solution.py:132
  30.4 0.0 collective-permute-done.3.above
  30.4 0.0 copy-start
  30.4 0.0 copy-start.1
  30.4 0.0 copy-start.2
  30.4 1.5 %shard_map.49 = bf16[8,64,768]{2,1,0:T(8,128)(2,1)S(1)} custom-call(f32[3,4,32,512]{3,2,1,0:T(8,128)S(1)} %get-tuple-element.17.now, bf16[8,32,512]{2,1,0:T(8,128)(2,1)S(1)} %collective-permute-done.2.below, bf16[8,32,512]{2,1,0:T(8,128)(2,1)S(1)} %collective-permute-done.3.above, ...), custom_call_target="tpu_custom_call", output_to_operand_aliasing={{}: (3, {})} | custom-call | flops 50000000 | bytes 1000000 | tf_op jit(solution)/shard_map/pallas_call | solution.py:142
  31.9 31.4 %all_to_all.10 = bf16[8,64,768]{2,1,0:T(8,128)(2,1)S(1)} all-to-all(bf16[8,64,768]{2,1,0:T(8,128)(2,1)S(1)} %shard_map.49), channel_id=1, replica_groups=mesh['member'=8,'space'=16,'group'=2] {'member'}, dimensions={0} | all-to-all | bytes 1572864 | tf_op jit(solution)/shard_map/all_to_all | solution.py:502
  63.3 0.0 copy-done
  63.3 0.0 copy-done.1
  63.3 0.0 copy-done.2
  63.3 6.2 %weights.1.refs_2_ = bf16[1168,128]{1,0:T(8,128)(2,1)S(1)} custom-call(bf16[512,768]{1,0:T(8,128)(2,1)S(1)} %bitcast.35, s32[1]{0:T(128)} %bitcast.16.refs_1_, s32[8,256]{1,0:T(8,128)S(1)} %bitcast.37, f32[1,256]{1,0:T(1,128)S(1)} %bitcast.38, f32[1,256]{1,0:T(1,128)S(1)} %bitcast.39), custom_call_target="tpu_custom_call" | custom-call | flops 6000000000 | bytes 1000000 | tf_op jit(solution)/shard_map/weights/pallas_call | solution.py:312
  69.5 0.1 collective-permute-start.10
  69.6 5.1 %collective-permute-start.11 = (bf16[1168,128]{1,0:T(8,128)(2,1)S(1)}, bf16[1168,128]{1,0:T(8,128)(2,1)S(1)}, u32[]{:S(2)}, u32[]{:S(2)}) collective-permute-start(bf16[1168,128]{1,0:T(8,128)(2,1)S(1)} %weights.1.refs_2_), channel_id=1, source_target_pairs={{2,0},{4,2},{6,4},{8,6},{10,8},{12,10},{14,12},{16,14},{18,16},{20... | collective-permute-start | bytes 897032 | tf_op jit(solution)/shard_map/ppermute | solution.py:508
  74.7 4.4 %collective-permute-start.9 = (bf16[1168,128]{1,0:T(8,128)(2,1)S(1)}, bf16[1168,128]{1,0:T(8,128)(2,1)S(1)}, u32[]{:S(2)}, u32[]{:S(2)}) collective-permute-start(bf16[1168,128]{1,0:T(8,128)(2,1)S(1)} %weights.1.refs_2_), channel_id=1, source_target_pairs={{0,224},{32,64},{64,32},{96,128},{128,96},{160,192},{192,160},{224... | collective-permute-start | bytes 897032 | tf_op jit(solution)/shard_map/ppermute | solution.py:506
  79.1 0.0 collective-permute-start.8
  79.1 0.0 collective-permute-done.10.below
  79.1 4.2 %collective-permute-start.12 = (bf16[1168,128]{1,0:T(8,128)(2,1)S(1)}, bf16[1168,128]{1,0:T(8,128)(2,1)S(1)}, u32[]{:S(2)}, u32[]{:S(2)}) collective-permute-start(bf16[1168,128]{1,0:T(8,128)(2,1)S(1)} %collective-permute-done.10.below), channel_id=1, source_target_pairs={{0,32},{32,0},{64,96},{96,64},{128,160},{160,128},{192,224},{224,1... | collective-permute-start | bytes 897032 | tf_op jit(solution)/shard_map/ppermute | solution.py:512
  83.3 0.0 collective-permute-done.11.above
  83.3 0.0 collective-permute-start.13
  83.3 3.8 %collective-permute-done.9.other = bf16[1168,128]{1,0:T(8,128)(2,1)S(1)} collective-permute-done((bf16[1168,128]{1,0:T(8,128)(2,1)S(1)}, bf16[1168,128]{1,0:T(8,128)(2,1)S(1)}, u32[]{:S(2)}, u32[]{:S(2)}) %collective-permute-start.9) | collective-permute-done | bytes 299040 | tf_op jit(solution)/shard_map/ppermute | solution.py:506
  87.1 0.0 collective-permute-start.14
  87.1 4.8 %collective-permute-start.15 = (bf16[1168,128]{1,0:T(8,128)(2,1)S(1)}, bf16[1168,128]{1,0:T(8,128)(2,1)S(1)}, u32[]{:S(2)}, u32[]{:S(2)}) collective-permute-start(bf16[1168,128]{1,0:T(8,128)(2,1)S(1)} %collective-permute-done.9.other), channel_id=1, source_target_pairs={{2,0},{4,2},{6,4},{8,6},{10,8},{12,10},{14,12},{16,14},{18,16},{20... | collective-permute-start | bytes 897032 | tf_op jit(solution)/shard_map/ppermute | solution.py:511
  91.9 1.2 shard_map.50
  93.1 0.0 collective-permute-done.8.sibling
  93.1 2.9 %shard_map.51.acc_in = f32[512,768]{1,0:T(8,128)S(1)} custom-call(s32[1]{0:T(128)} %bitcast.2.refs_0_.parity, f32[512,768]{1,0:T(8,128)S(1)} %get-tuple-element.23.acc_in, bf16[512,768]{1,0:T(8,128)(2,1)S(1)} %get-tuple-element.24.dev, bf16[1168,128]{1,0:T(8,128)(2,1)S(1)} %collective-permute-done.8.sibling, ...), custom_call_target="tpu_custom_call", output_to_operand_aliasing={{}: (1, {})} | custom-call | flops 1200000000 | bytes 1000000 | tf_op jit(solution)/shard_map/pallas_call | solution.py:439
  96.0 0.0 collective-permute-done.12.below_sibling
  96.0 0.0 collective-permute-done.13.above_sibling
  96.0 1.1 shard_map.52.acc
  97.2 0.0 collective-permute-done.14.below_other
  97.2 0.0 collective-permute-done.15.above_other
  97.2 1.2 shard_map.53
  98.4 27.5 %all_to_all.11.back = bf16[8,64,768]{2,1,0:T(8,128)(2,1)S(1)} all-to-all(bf16[8,64,768]{2,1,0:T(8,128)(2,1)S(1)} %shard_map.53), channel_id=1, replica_groups=mesh['member'=8,'space'=16,'group'=2] {'member'}, dimensions={0} | all-to-all | bytes 1572864 | tf_op jit(solution)/shard_map/all_to_all | solution.py:522
  125.9 1.6 %restore.1 = bf16[1,64,3,4,512]{4,3,2,1,0:T(4,128)(2,1)} custom-call(bf16[8,64,768]{2,1,0:T(8,128)(2,1)S(1)} %all_to_all.11.back), custom_call_target="tpu_custom_call" | custom-call | flops 10000000 | bytes 1000000 | tf_op jit(solution)/shard_map/restore/pallas_call | solution.py:477
  (5 shorter events, 0.2 us)
Async XLA Ops:
  1.5 10.0 %collective-permute-start.4 = (bf16[8,32,512]{2,1,0:T(8,128)(2,1)S(1)}, bf16[8,32,512]{2,1,0:T(8,128)(2,1)S(1)}, u32[]{:S(2)}, u32[]{:S(2)}) collective-permute-start(bf16[8,32,512]{2,1,0:T(8,128)(2,1)S(1)} %pad_maximum_fusion.2), channel_id=1, source_target_pairs={{0,2},{2,4},{4,6},{6,8},{8,10},{10,12},{12,14},{14,16},{16,18},{18... | collective-permute-start | bytes 786440 | tf_op jit(solution)/shard_map/ppermute | solution.py:132
  3.7 7.8 %collective-permute-start.5 = (bf16[8,32,512]{2,1,0:T(8,128)(2,1)S(1)}, bf16[8,32,512]{2,1,0:T(8,128)(2,1)S(1)}, u32[]{:S(2)}, u32[]{:S(2)}) collective-permute-start(bf16[8,32,512]{2,1,0:T(8,128)(2,1)S(1)} %pad_maximum_fusion.3), channel_id=1, source_target_pairs={{2,0},{4,2},{6,4},{8,6},{10,8},{12,10},{14,12},{16,14},{18,16},{20... | collective-permute-start | bytes 786440 | tf_op jit(solution)/shard_map/ppermute | solution.py:132
  7.5 10.2 %collective-permute-start.1 = (bf16[8,32,512]{2,1,0:T(8,128)(2,1)S(1)}, bf16[8,32,512]{2,1,0:T(8,128)(2,1)S(1)}, u32[]{:S(2)}, u32[]{:S(2)}) collective-permute-start(bf16[8,32,512]{2,1,0:T(8,128)(2,1)S(1)} %pad_maximum_fusion.1), channel_id=1, source_target_pairs={{2,0},{4,2},{6,4},{8,6},{10,8},{12,10},{14,12},{16,14},{18,16},{20... | collective-permute-start | bytes 786440 | tf_op jit(solution)/shard_map/ppermute | solution.py:132
  9.0 9.7 %collective-permute-start = (bf16[8,32,512]{2,1,0:T(8,128)(2,1)S(1)}, bf16[8,32,512]{2,1,0:T(8,128)(2,1)S(1)}, u32[]{:S(2)}, u32[]{:S(2)}) collective-permute-start(bf16[8,32,512]{2,1,0:T(8,128)(2,1)S(1)} %pad_maximum_fusion), channel_id=1, source_target_pairs={{0,2},{2,4},{4,6},{6,8},{8,10},{10,12},{12,14},{14,16},{16,18},{18... | collective-permute-start | bytes 786440 | tf_op jit(solution)/shard_map/ppermute | solution.py:132
  12.8 12.2 %collective-permute-start.6 = (bf16[8,32,512]{2,1,0:T(8,128)(2,1)S(1)}, bf16[8,32,512]{2,1,0:T(8,128)(2,1)S(1)}, u32[]{:S(2)}, u32[]{:S(2)}) collective-permute-start(bf16[8,32,512]{2,1,0:T(8,128)(2,1)S(1)} %get-tuple-element.21), channel_id=1, source_target_pairs={{0,2},{2,4},{4,6},{6,8},{8,10},{10,12},{12,14},{14,16},{16,18},{18... | collective-permute-start | bytes 786440 | tf_op jit(solution)/shard_map/ppermute | solution.py:132
  13.4 11.6 %collective-permute-start.7 = (bf16[8,32,512]{2,1,0:T(8,128)(2,1)S(1)}, bf16[8,32,512]{2,1,0:T(8,128)(2,1)S(1)}, u32[]{:S(2)}, u32[]{:S(2)}) collective-permute-start(bf16[8,32,512]{2,1,0:T(8,128)(2,1)S(1)} %get-tuple-element.22), channel_id=1, source_target_pairs={{2,0},{4,2},{6,4},{8,6},{10,8},{12,10},{14,12},{16,14},{18,16},{20... | collective-permute-start | bytes 786440 | tf_op jit(solution)/shard_map/ppermute | solution.py:132
  20.1 10.3 %collective-permute-start.2 = (bf16[8,32,512]{2,1,0:T(8,128)(2,1)S(1)}, bf16[8,32,512]{2,1,0:T(8,128)(2,1)S(1)}, u32[]{:S(2)}, u32[]{:S(2)}) collective-permute-start(bf16[8,32,512]{2,1,0:T(8,128)(2,1)S(1)} %get-tuple-element.18), channel_id=1, source_target_pairs={{0,2},{2,4},{4,6},{6,8},{8,10},{10,12},{12,14},{14,16},{16,18},{18... | collective-permute-start | bytes 786440 | tf_op jit(solution)/shard_map/ppermute | solution.py:132
  20.1 10.3 %collective-permute-start.3 = (bf16[8,32,512]{2,1,0:T(8,128)(2,1)S(1)}, bf16[8,32,512]{2,1,0:T(8,128)(2,1)S(1)}, u32[]{:S(2)}, u32[]{:S(2)}) collective-permute-start(bf16[8,32,512]{2,1,0:T(8,128)(2,1)S(1)} %get-tuple-element.19), channel_id=1, source_target_pairs={{2,0},{4,2},{6,4},{8,6},{10,8},{12,10},{14,12},{16,14},{18,16},{20... | collective-permute-start | bytes 786440 | tf_op jit(solution)/shard_map/ppermute | solution.py:132
  30.4 32.9 %copy-start = (s32[1,1,8,256]{3,2,1,0:T(8,128)S(1)}, s32[1,1,8,256]{3,2,1,0:T(8,128)}, u32[]{:S(2)}) copy-start(s32[1,1,8,256]{3,2,1,0:T(8,128)} %param.5) | copy-start | bytes 24580
  30.4 32.9 %copy-start.1 = (f32[1,1,1,256]{3,2,1,0:T(1,128)S(1)}, f32[1,1,1,256]{3,2,1,0:T(1,128)}, u32[]{:S(2)}) copy-start(f32[1,1,1,256]{3,2,1,0:T(1,128)} %param.6) | copy-start | bytes 3076
  30.4 32.9 %copy-start.2 = (f32[1,1,1,256]{3,2,1,0:T(1,128)S(1)}, f32[1,1,1,256]{3,2,1,0:T(1,128)}, u32[]{:S(2)}) copy-start(f32[1,1,1,256]{3,2,1,0:T(1,128)} %param.7) | copy-start | bytes 3076
  69.5 9.6 %collective-permute-start.10 = (bf16[1168,128]{1,0:T(8,128)(2,1)S(1)}, bf16[1168,128]{1,0:T(8,128)(2,1)S(1)}, u32[]{:S(2)}, u32[]{:S(2)}) collective-permute-start(bf16[1168,128]{1,0:T(8,128)(2,1)S(1)} %weights.1.refs_2_), channel_id=1, source_target_pairs={{0,2},{2,4},{4,6},{6,8},{8,10},{10,12},{12,14},{14,16},{16,18},{18... | collective-permute-start | bytes 897032 | tf_op jit(solution)/shard_map/ppermute | solution.py:507
  69.6 13.7 %collective-permute-start.11 = (bf16[1168,128]{1,0:T(8,128)(2,1)S(1)}, bf16[1168,128]{1,0:T(8,128)(2,1)S(1)}, u32[]{:S(2)}, u32[]{:S(2)}) collective-permute-start(bf16[1168,128]{1,0:T(8,128)(2,1)S(1)} %weights.1.refs_2_), channel_id=1, source_target_pairs={{2,0},{4,2},{6,4},{8,6},{10,8},{12,10},{14,12},{16,14},{18,16},{20... | collective-permute-start | bytes 897032 | tf_op jit(solution)/shard_map/ppermute | solution.py:508
  74.7 12.4 %collective-permute-start.9 = (bf16[1168,128]{1,0:T(8,128)(2,1)S(1)}, bf16[1168,128]{1,0:T(8,128)(2,1)S(1)}, u32[]{:S(2)}, u32[]{:S(2)}) collective-permute-start(bf16[1168,128]{1,0:T(8,128)(2,1)S(1)} %weights.1.refs_2_), channel_id=1, source_target_pairs={{0,224},{32,64},{64,32},{96,128},{128,96},{160,192},{192,160},{224... | collective-permute-start | bytes 897032 | tf_op jit(solution)/shard_map/ppermute | solution.py:506
  79.1 14.0 %collective-permute-start.8 = (bf16[1168,128]{1,0:T(8,128)(2,1)S(1)}, bf16[1168,128]{1,0:T(8,128)(2,1)S(1)}, u32[]{:S(2)}, u32[]{:S(2)}) collective-permute-start(bf16[1168,128]{1,0:T(8,128)(2,1)S(1)} %weights.1.refs_2_), channel_id=1, source_target_pairs={{0,32},{32,0},{64,96},{96,64},{128,160},{160,128},{192,224},{224,1... | collective-permute-start | bytes 897032 | tf_op jit(solution)/shard_map/ppermute | solution.py:509
  79.1 16.9 %collective-permute-start.12 = (bf16[1168,128]{1,0:T(8,128)(2,1)S(1)}, bf16[1168,128]{1,0:T(8,128)(2,1)S(1)}, u32[]{:S(2)}, u32[]{:S(2)}) collective-permute-start(bf16[1168,128]{1,0:T(8,128)(2,1)S(1)} %collective-permute-done.10.below), channel_id=1, source_target_pairs={{0,32},{32,0},{64,96},{96,64},{128,160},{160,128},{192,224},{224,1... | collective-permute-start | bytes 897032 | tf_op jit(solution)/shard_map/ppermute | solution.py:512
  83.3 12.7 %collective-permute-start.13 = (bf16[1168,128]{1,0:T(8,128)(2,1)S(1)}, bf16[1168,128]{1,0:T(8,128)(2,1)S(1)}, u32[]{:S(2)}, u32[]{:S(2)}) collective-permute-start(bf16[1168,128]{1,0:T(8,128)(2,1)S(1)} %collective-permute-done.11.above), channel_id=1, source_target_pairs={{0,32},{32,0},{64,96},{96,64},{128,160},{160,128},{192,224},{224,1... | collective-permute-start | bytes 897032 | tf_op jit(solution)/shard_map/ppermute | solution.py:513
  87.1 10.1 %collective-permute-start.14 = (bf16[1168,128]{1,0:T(8,128)(2,1)S(1)}, bf16[1168,128]{1,0:T(8,128)(2,1)S(1)}, u32[]{:S(2)}, u32[]{:S(2)}) collective-permute-start(bf16[1168,128]{1,0:T(8,128)(2,1)S(1)} %collective-permute-done.9.other), channel_id=1, source_target_pairs={{0,2},{2,4},{4,6},{6,8},{8,10},{10,12},{12,14},{14,16},{16,18},{18... | collective-permute-start | bytes 897032 | tf_op jit(solution)/shard_map/ppermute | solution.py:510
  87.1 10.1 %collective-permute-start.15 = (bf16[1168,128]{1,0:T(8,128)(2,1)S(1)}, bf16[1168,128]{1,0:T(8,128)(2,1)S(1)}, u32[]{:S(2)}, u32[]{:S(2)}) collective-permute-start(bf16[1168,128]{1,0:T(8,128)(2,1)S(1)} %collective-permute-done.9.other), channel_id=1, source_target_pairs={{2,0},{4,2},{6,4},{8,6},{10,8},{12,10},{14,12},{16,14},{18,16},{20... | collective-permute-start | bytes 897032 | tf_op jit(solution)/shard_map/ppermute | solution.py:511
